TPU v7x, 32 devices: a whole 2x2x4 slice. The times are simulated.
32 devices in a mesh: dp: 8 (over z, y), tensor: 4 (over x, core).
Axes of the slice: x: 2, y: 2, z: 4, core: 2. Of those that a mesh axis runs over, the one named last changes fastest.
Arguments:
- hidden_in: bfloat16 [256, 4096], P('dp'), may hold values from -6 to 6
- norm_gain: float32 [4096], replicated, may hold values from 0.5 to 1.5
- w_in: bfloat16 [4096, 2, 4, 2048], P(None, None, 'tensor', 'dp'), may hold values from -0.09375 to 0.09375
- conv_w: float32 [4, 8192], P(None, 'tensor'), may hold values from -3 to 3
- conv_b: float32 [8192], P('tensor'), may hold values from -2 to 2
- w_dt_low: bfloat16 [8192, 256], P('tensor'), may hold values from -0.0625 to 0.0625
- w_bc: bfloat16 [32, 8192], P(None, 'tensor'), may hold values from -0.0625 to 0.0625
- w_dt: bfloat16 [256, 8192], P(None, 'tensor'), may hold values from -0.375 to 0.375
- dt_bias: float32 [8192], P('tensor'), may hold values from -5 to -1.5
- a_log: float32 [16, 8192], P(None, 'tensor'), may hold values from 0 to 2.77
- d_skip: float32 [8192], P('tensor'), may hold values from 0.5 to 1.5
- w_out: bfloat16 [8192, 4096], P('tensor', 'dp'), may hold values from -0.0625 to 0.0625
- conv_state: bfloat16 [256, 3, 8192], P('dp', None, 'tensor'), may hold values from -6 to 6
- ssm_state: float32 [256, 16, 8192], P('dp', None, 'tensor'), may hold values from -6 to 6
- lengths: int32 [256], P('dp'), may hold values from 0 to 5
- active_ids: int32 [8, 32], P('dp'), may hold values from 0 to 31, each once within a row
- active_count: int32 [8], P('dp'), may hold values from 1 to 24, as said below
Outputs:
- mixed: bfloat16 [256, 4096], P('dp', 'tensor')
- conv_next: bfloat16 [256, 3, 8192], P('dp', None, 'tensor')
- ssm_next: float32 [256, 16, 8192], P('dp', None, 'tensor')
Inputs may be any that keep to these rules, and one draw needn't show every extreme that they name: `active_count`: at most 24 slots of a dp index are active; some dp index has exactly 24. `active_ids`: each row lists every slot 0 to 31 of its dp index once.
All inputs are finite; a program needn't handle non-finite values.
Results may differ from a plain program's by a relative error of at most 0.014.
Values may be sent and summed in bfloat16 or wider, within the bound.
No kernel may reach another device: no remote copies, remote signals or barrier semaphores. Data moves between devices by JAX's collectives and lax.ppermute only.
A program may use at most 128 MiB of HBM per device.

v0:
```python
import jax
import jax.numpy as jnp
from jax import lax
from jax.experimental import pallas as pl
from jax.experimental.pallas import tpu as pltpu
from jax.sharding import PartitionSpec as P


ACT_MAX = 24


F32 = jnp.float32
BF16 = jnp.bfloat16
VMEM = pl.BlockSpec(memory_space=pltpu.VMEM)
SMEM = pl.BlockSpec(memory_space=pltpu.SMEM)
HBM = pl.BlockSpec(memory_space=pltpu.HBM)


def near(values):
    return pltpu.with_memory_space_constraint(values, pltpu.VMEM)


def small(values):
    return pltpu.with_memory_space_constraint(values, pltpu.SMEM)


def away(values):
    return pltpu.with_memory_space_constraint(values, pltpu.HBM)


def limit(mebibytes):
    return pltpu.CompilerParams(vmem_limit_bytes=mebibytes * 1024 * 1024)


def rms_rows(values, epsilon):
    return values * lax.rsqrt(jnp.mean(values * values, axis=-1, keepdims=True) + epsilon)


def silu(values):
    return values / (1.0 + jnp.exp(-values))


def iota(shape, dim):
    return lax.broadcasted_iota(jnp.int32, shape, dim)


def norm_kernel(ids_hbm, hidden_hbm, gain_hbm, chosen, ids, hidden, gain, sems):
    pairs = ((ids_hbm, ids), (hidden_hbm, hidden), (gain_hbm, gain))
    copies = [pltpu.make_async_copy(a, b, sems.at[i]) for i, (a, b) in enumerate(pairs)]
    for copy in copies:
        copy.start()
    rows, slots = chosen.shape[0], hidden.shape[0]
    at = iota((rows, slots), 0), iota((rows, slots), 1)
    one_hot = jnp.zeros((rows, slots), F32)
    copies[0].wait()
    for j in range(rows):
        one_hot = jnp.where((at[0] == j) & (at[1] == ids[0, j]), 1.0, one_hot)
    for copy in copies[1:]:
        copy.wait()
    values = jnp.dot(one_hot.astype(BF16), hidden[...], preferred_element_type=F32)
    chosen[...] = (rms_rows(values, 1e-05) * gain[...]).astype(BF16)


def spread_matrix(ids, count, shape):
    at = iota(shape, 0), iota(shape, 1)
    live = jnp.zeros(shape, F32)
    for j in range(shape[1]):
        early = jnp.where(j < count[0], 1.0, 0.0)
        live = jnp.where((at[1] == j) & (at[0] == ids[0, j]), early, live)
    return live


def pick_matrix(ids, shape):
    at = iota(shape, 0), iota(shape, 1)
    one_hot = jnp.zeros(shape, F32)
    for j in range(shape[0]):
        one_hot = jnp.where((at[0] == j) & (at[1] == ids[0, j]), 1.0, one_hot)
    return one_hot


def prefetch_kernel(*refs, parts):
    sources, targets, sems = refs[:parts], refs[parts + 1 :][-parts - 1 : -1], refs[-1]
    extra = refs[parts + 1 : -parts - 1]
    copies = [
        pltpu.make_async_copy(a, b, sems.at[i]) for i, (a, b) in enumerate(zip(sources, targets))
    ]
    for copy in copies:
        copy.start()
    if extra:
        ids, count, spread, pick, live = extra
        matrix = spread_matrix(ids, count, spread.shape)
        spread[...] = matrix.astype(BF16)
        live[...] = jnp.sum(matrix, axis=1, keepdims=True)
        pick[...] = pick_matrix(ids, pick.shape).astype(BF16)
    for copy in copies:
        copy.wait()


def input_kernel(*refs, parts):
    own, place = refs[0][0], refs[1][0]
    blocks = refs[2 : 2 + parts]
    weights_hbm, branches, stacked, weights, sems = refs[2 + parts :]
    rows = blocks[0].shape[0]
    chunks = sems.shape[0]
    deep = weights.shape[0] // chunks
    pieces = [slice(i * deep, (i + 1) * deep) for i in range(chunks)]
    copies = [
        pltpu.make_async_copy(weights_hbm.at[at, :], weights.at[at, :], sems.at[i])
        for i, at in enumerate(pieces)
    ]
    for copy in copies:
        copy.start()
    for k, ref in enumerate(blocks):
        stacked[k * rows : (k + 1) * rows, :] = ref[...]
    result = None
    for copy, at in zip(copies, pieces):
        copy.wait()
        part = jnp.dot(stacked[:, at], weights[at, :], preferred_element_type=F32)
        result = part if result is None else result + part
    for k in range(parts):
        mask = jnp.where(place % 2 == 0, *SHARED_MASKS[k])
        branches[own ^ mask] = result[k * rows : (k + 1) * rows, :].astype(BF16)


def filter_kernel(spread, x_new, z_new, lengths, conv_state, conv_w, conv_b, w_dt_low, w_bc,
                  packed, filtered, x_in, z_in):
    taps = conv_w.shape[0]

    def branch(ref, first):
        if len(ref.shape) == 2:
            return ref[...]
        block = ref.shape[2] // 2
        parts = [ref[k, :, first * block : (first + 1) * block] for k in range(ref.shape[0])]
        return jnp.concatenate(parts, axis=1)

    def to_slots(values):
        return jnp.dot(spread[...], values, preferred_element_type=F32)

    x_slots = to_slots(branch(x_new, 0))
    x_in[...] = x_slots.astype(BF16)
    known = lengths[...]
    total = conv_w[taps - 1 : taps, :] * x_slots * (known >= 0).astype(F32)
    for k in range(taps - 1):
        usable = (known >= taps - 1 - k).astype(F32)
        total = total + conv_w[k : k + 1, :] * conv_state[k].astype(F32) * usable
    result = silu(total + conv_b[...]).astype(BF16)
    filtered[...] = result
    rank = w_dt_low.shape[1]
    packed[:, :rank] = jnp.dot(result, w_dt_low[...], preferred_element_type=F32)
    packed[:, rank:] = lax.dot_general(
        result, w_bc[...], (((1,), (1,)), ((), ())), preferred_element_type=F32
    )
    z_in[...] = to_slots(branch(z_new, 1)).astype(BF16)


def state_kernel(*refs, parts, group, wide):
    sums = refs[:parts]
    (pick, live, w_dt, dt_bias, a_log, d_skip, filtered, z_in, lengths, states,
     gated, states_next,
     result, step, drive, b_wide, c_wide, decay, pieces, out_sem) = refs[parts:]
    count = a_log.shape[0]
    slots, width = filtered.shape
    chunks = slots // group
    tiles = width // 128
    halves = count // 8
    span = group * halves * tiles * 8

    def save(k):
        piece = pl.ds(k * span, span)
        return pltpu.make_async_copy(result.at[piece], states_next.at[piece], out_sem.at[k])

    active = live[...] > 0.5
    total = sums[0][...]
    for other in sums[1:]:
        total = total + other[...]
    rank = w_dt.shape[0]
    low = rms_rows(total[:, :rank], 1e-06).astype(BF16)
    b_in = rms_rows(total[:, rank : rank + count], 1e-06)
    c_out = rms_rows(total[:, rank + count : rank + 2 * count], 1e-06)
    raw = jnp.dot(low, w_dt[...], preferred_element_type=F32) + dt_bias[...]
    size = jnp.maximum(raw, 0.0) + jnp.log1p(jnp.exp(-jnp.abs(raw)))
    fresh = lengths[...] > 0
    step[...] = jnp.where(active, jnp.where(fresh, size, 1e30), 0.0)
    drive[...] = jnp.where(active, size * filtered[...].astype(F32), 0.0)
    decay[...] = jnp.exp(a_log[...]) * -1.4426950408889634
    for n in range(count):
        at = pl.ds(n, slots, stride=count)
        b_wide[at, :] = jnp.broadcast_to(b_in[:, n : n + 1], (slots, 128))
        c_wide[at, :] = jnp.broadcast_to(c_out[:, n : n + 1], (slots, 128))
    for k in range(chunks):

        def column(i, carry):
            for u in range(wide):
                tile = i * wide + u
                lanes = pl.ds(pl.multiple_of(tile * 128, 128), 128)
                rates = [decay[h * 8 : h * 8 + 8, lanes] for h in range(halves)]
                for r in range(k * group, (k + 1) * group):
                    size = step[r : r + 1, lanes]
                    push = drive[r : r + 1, lanes]
                    y = None
                    for h in range(halves):
                        first = (r * halves + h) * tiles * 8 + tile * 8
                        at = pl.ds(pl.multiple_of(first, 8), 8)
                        own = slice(r * count + h * 8, r * count + h * 8 + 8)
                        new = jnp.exp2(size * rates[h]) * states[at, :] + push * b_wide[own, :]
                        result[at, :] = new
                        part = c_wide[own, :] * new
                        y = part if y is None else y + part
                    pieces[pl.ds(pl.multiple_of((tile * slots + r) * 8, 8), 8), :] = y
            return carry

        lax.fori_loop(0, tiles // wide, column, 0)
        save(k).start()
    outputs = []
    for tile in range(tiles):
        y = pieces[pl.ds(tile * slots * 8, slots, stride=8), :]
        for n in range(1, 8):
            y = y + pieces[pl.ds(tile * slots * 8 + n, slots, stride=8), :]
        outputs.append(y)
    filt = filtered[...].astype(F32)
    mixed = jnp.concatenate(outputs, axis=1) + d_skip[...] * filt
    mixed = (mixed * silu(z_in[...].astype(F32))).astype(BF16)
    gated[...] = jnp.dot(pick[...], mixed, preferred_element_type=F32).astype(BF16)
    for k in range(chunks):
        save(k).wait()


def mix_kernel(spread, columns, first, second, mixed):
    half = first.shape[1]
    matrix = spread[...]
    for i, ref in enumerate((first, second)):
        lanes = slice(i * half, (i + 1) * half)
        added = jnp.dot(matrix, ref[...], preferred_element_type=F32)
        mixed[:, lanes] = (columns[:, lanes].astype(F32) + added).astype(BF16)


def swap_by(values, axis, size, mask):
    return lax.ppermute(values, axis, [(i, i ^ mask) for i in range(size)])


def swap_by_core(values, n_dp, n_t, masks):
    perm = []
    for g in range(n_dp):
        for t in range(n_t):
            perm.append(((g ^ masks[t % 2]) * n_t + t, g * n_t + t))
    return lax.ppermute(values, ("dp", "tensor"), perm)


SHARED_MASKS = ((0, 0), (1, 1), (4, 2), (5, 3), (6, 7), (2, 4), (3, 5), (7, 6))


def gather_shared(block, weights, t, n_dp, n_t):
    even = t % 2 == 0
    side = swap_by_core(block, n_dp, n_t, (1, 1))
    far = swap_by_core(block, n_dp, n_t, (4, 2))
    far_side = swap_by_core(far, n_dp, n_t, (1, 1))
    last = swap_by_core(jnp.where(even, far, side), n_dp, n_t, (2, 6))
    weights, far = lax.optimization_barrier((weights, far))
    weights = weights.reshape(weights.shape[0], -1)
    weights, far_side, last = lax.optimization_barrier((weights, far_side, last))
    swapped = [swap_by(v, "tensor", n_t, 1) for v in (far, far_side, last)]
    return weights, [block, side, far, far_side, last] + swapped


def gather_own(block, g, n_dp):
    far, near, side = (swap_by(block, "dp", n_dp, m) for m in (4, 2, 1))
    both = swap_by(far, "dp", n_dp, 2)
    near_side = swap_by(near, "dp", n_dp, 1)
    far_side = swap_by(far, "dp", n_dp, 1)
    both_side = swap_by(side, "dp", n_dp, 6)
    blocks = [block, side, near, near_side, far, far_side, both, both_side]
    return blocks, [g ^ k for k in range(n_dp)]


def in_order(blocks, places):
    stacked = jnp.zeros((len(blocks),) + blocks[0].shape, blocks[0].dtype)
    for place, block in zip(places, blocks):
        stacked = lax.dynamic_update_index_in_dim(stacked, block, place, 0)
    return stacked.reshape(-1, blocks[0].shape[1])


def make_body(n_dp, n_t):
    direct = n_dp == 8 and n_t == 4

    def body(hidden_in, norm_gain, w_in, conv_w, conv_b, w_dt_low, w_bc, w_dt, dt_bias, a_log,
             d_skip, w_out, conv_state, ssm_state, lengths, active_ids, active_count):
        slots, depth = hidden_in.shape
        rows = min(ACT_MAX, slots)
        share = depth // n_t
        width = conv_w.shape[1]
        block = w_in.shape[3]
        rank = w_dt_low.shape[1]
        count = a_log.shape[0]
        g = lax.axis_index("dp")
        t = lax.axis_index("tensor")

        def out(shape, dtype):
            return jax.ShapeDtypeStruct(shape, dtype)

        def near_out(shape, dtype):
            return pltpu.VMEM(shape, dtype)

        own, place = small(g[None].astype(jnp.int32)), small(t[None].astype(jnp.int32))
        ids, held = small(active_ids), small(active_count)
        chosen = pl.pallas_call(
            norm_kernel,
            out_shape=near_out((rows, depth), BF16),
            in_specs=[HBM] * 3,
            out_specs=VMEM,
            scratch_shapes=[
                pltpu.SMEM(active_ids.shape, jnp.int32),
                pltpu.VMEM(hidden_in.shape, BF16),
                pltpu.VMEM((1, depth), F32),
                pltpu.SemaphoreType.DMA((3,)),
            ],
            compiler_params=limit(4),
            name="norm",
        )(away(active_ids), away(hidden_in), away(norm_gain[None]))

        def prefetch(values, after, *matrices):
            return pl.pallas_call(
                lambda *refs: prefetch_kernel(*refs, parts=len(values)),
                out_shape=matrices + tuple(near_out(v.shape, v.dtype) for v in values),
                in_specs=[HBM] * len(values)
                + [pl.BlockSpec(memory_space=pl.ANY)]
                + [SMEM] * (2 if matrices else 0),
                out_specs=(VMEM,) * (len(values) + len(matrices)),
                scratch_shapes=[pltpu.SemaphoreType.DMA((len(values),))],
                compiler_params=limit(1),
                name="prefetch",
            )(*[away(v) for v in values], after, *((ids, held) if matrices else ()))

        if direct:
            weights, blocks = gather_shared(chosen, w_in, t, n_dp, n_t)
            branches = pl.pallas_call(
                lambda *refs: input_kernel(*refs, parts=n_dp),
                out_shape=out((n_dp, rows, 2 * block), BF16),
                in_specs=[SMEM] * 2 + [VMEM] * n_dp + [HBM],
                out_specs=VMEM,
                scratch_shapes=[
                    pltpu.VMEM((n_dp * rows, depth), BF16),
                    pltpu.VMEM(weights.shape, BF16),
                    pltpu.SemaphoreType.DMA((4,)),
                ],
                compiler_params=limit(12),
                name="input",
            )(own, place, *[near(b) for b in blocks], away(weights))
        else:
            full = lax.all_gather(chosen, "dp", axis=0, tiled=True)
            branches = jnp.dot(full, w_in.reshape(depth, 2 * block), preferred_element_type=F32)
            branches = branches.astype(BF16).reshape(n_dp, rows, 2 * block)
        owned = lax.all_to_all(branches, "dp", split_axis=0, concat_axis=0, tiled=True)
        past = jnp.transpose(conv_state, (1, 0, 2))
        flat = slots * count * width // 128
        states = ssm_state.reshape(slots, count // 8, 8, width // 128, 128)
        states = jnp.transpose(states, (0, 1, 3, 2, 4)).reshape(flat, 128)
        spread, pick, live, past_n, conv_w_n, conv_b_n, w_dt_low_n, w_bc_n = prefetch(
            (past, conv_w, conv_b[None], w_dt_low, w_bc),
            branches,
            near_out((slots, rows), BF16),
            near_out((rows, slots), BF16),
            near_out((slots, 1), F32),
        )
        if block % 128 == 0:
            x_new = z_new = owned
        else:
            owned = jnp.transpose(owned.reshape(n_dp, rows, 2, block), (2, 1, 0, 3))
            x_new, z_new = owned[0].reshape(rows, width), owned[1].reshape(rows, width)
        known = lengths[:, None]
        packed, filtered, x_in, z_in = pl.pallas_call(
            filter_kernel,
            out_shape=(
                near_out((slots, rank + 2 * count), F32),
                near_out((slots, width), BF16),
                near_out((slots, width), BF16),
                near_out((slots, width), BF16),
            ),
            in_specs=[VMEM] * 9,
            out_specs=(VMEM,) * 4,
            compiler_params=limit(8),
            name="filter",
        )(near(spread), near(x_new), near(z_new), near(known), near(past_n), near(conv_w_n),
          near(conv_b_n), near(w_dt_low_n), near(w_bc_n))
        if direct:
            sums = [packed] + [swap_by(packed, "tensor", n_t, m) for m in range(1, n_t)]
        else:
            sums = [lax.psum(packed, "tensor")]
        w_dt_n, bias_n, a_log_n, skip_n, states_n = prefetch(
            (w_dt, dt_bias[None], a_log, d_skip[None], states), packed
        )
        group, wide = 8, 2
        gated, states_next = pl.pallas_call(
            lambda *refs: state_kernel(*refs, parts=len(sums), group=group, wide=wide),
            out_shape=(near_out((rows, width), BF16), out((flat, 128), F32)),
            in_specs=[VMEM] * (len(sums) + 10),
            out_specs=(VMEM, HBM),
            scratch_shapes=[
                pltpu.VMEM((flat, 128), F32),
                pltpu.VMEM((slots, width), F32),
                pltpu.VMEM((slots, width), F32),
                pltpu.VMEM((slots * count, 128), F32),
                pltpu.VMEM((slots * count, 128), F32),
                pltpu.VMEM((count, width), F32),
                pltpu.VMEM((slots * width // 16, 128), F32),
                pltpu.SemaphoreType.DMA((slots // group,)),
            ],
            compiler_params=limit(12),
            name="state",
        )(*[near(v) for v in sums], near(pick), near(live), near(w_dt_n), near(bias_n), near(a_log_n),
          near(skip_n), near(filtered), near(z_in), near(known), near(states_n))
        states_next = states_next.reshape(slots, count // 8, width // 128, 8, 128)
        states_next = jnp.transpose(states_next, (0, 1, 3, 2, 4))
        early = jnp.arange(slots, dtype=jnp.int32) < active_count[0]
        hits = (active_ids[0][:, None] == jnp.arange(slots, dtype=jnp.int32)[None, :]) & early[:, None]
        kept = jnp.any(hits, axis=0)
        moved = jnp.concatenate([past[1:], x_in[None]], axis=0)
        conv_next = jnp.transpose(jnp.where(kept[None, :, None], moved, past), (1, 0, 2))
        hidden_columns = lax.dynamic_slice_in_dim(hidden_in, t * share, share, 1)
        if direct:
            blocks, places = gather_own(gated, g, n_dp)
            w_out_n, columns = prefetch((w_out, hidden_columns), gated)
            partial = jnp.dot(in_order(blocks, places), w_out_n, preferred_element_type=F32)
            partial = partial.astype(BF16)
            base = 2 * (t ^ 2)
            pieces = [
                lax.dynamic_slice_in_dim(partial, (base ^ (2 * m)) * rows, 2 * rows, 0)
                for m in range(n_t)
            ]
            total = pieces[0].astype(F32)
            for m in range(1, n_t):
                total = total + swap_by(pieces[m], "tensor", n_t, m).astype(F32)
            total = total.astype(BF16)
            side = g % 2
            got = []
            for k in range(2):
                perm = []
                for gg in range(n_dp):
                    for tt in range(n_t):
                        dest = 2 * (tt ^ 2) + ((gg % 2) ^ k)
                        perm.append((gg * n_t + tt, dest * n_t + gg // 2))
                sent = lax.dynamic_slice_in_dim(total, (side ^ k) * rows, rows, 0)
                got.append(lax.ppermute(sent, ("dp", "tensor"), perm))
            first = jnp.where(side == 0, got[0], got[1])
            second = jnp.where(side == 0, got[1], got[0])
        else:
            _, columns = prefetch((w_out, hidden_columns), gated)
            gathered = lax.all_gather(gated, "dp", axis=0, tiled=True)
            partial = jnp.dot(gathered, w_out, preferred_element_type=F32).astype(BF16)
            by_sequence = lax.all_to_all(partial, "dp", split_axis=0, concat_axis=1, tiled=True)
            summed = lax.psum_scatter(by_sequence, "tensor", scatter_dimension=1, tiled=True)
            first, second = summed[:, : share // 2], summed[:, share // 2 :]
        mixed = pl.pallas_call(
            mix_kernel,
            out_shape=out((slots, share), BF16),
            in_specs=[VMEM] * 4,
            out_specs=VMEM,
            compiler_params=limit(2),
            name="mix",
        )(near(spread), near(columns), near(first), near(second))
        return mixed, conv_next, states_next.reshape(slots, count, width)

    return body


def solution(mesh):
    in_specs = (
        P("dp", None),
        P(),
        P(None, None, "tensor", "dp"),
        P(None, "tensor"),
        P("tensor"),
        P("tensor", None),
        P(None, "tensor"),
        P(None, "tensor"),
        P("tensor"),
        P(None, "tensor"),
        P("tensor"),
        P("tensor", "dp"),
        P("dp", None, "tensor"),
        P("dp", None, "tensor"),
        P("dp"),
        P("dp", None),
        P("dp"),
    )
    out_specs = (P("dp", "tensor"), P("dp", None, "tensor"), P("dp", None, "tensor"))
    inner = make_body(mesh.shape["dp"], mesh.shape["tensor"])

    return jax.shard_map(inner, mesh=mesh, in_specs=in_specs, out_specs=out_specs, check_vma=False)
```

profile of v0, /device:TPU:0, one launch (start us, length us, event | category | flops | bytes accessed | tf_op | source)
XLA Modules:
  0.0 76.9 jit_solution(8568977509313475729)
XLA Ops:
  0.6 1.3 %norm.1.refs_2_ = bf16[24,4096]{1,0:T(8,128)(2,1)S(1)} custom-call(s32[1,32]{1,0:T(1,128)} %refs_6_.1, bf16[32,4096]{1,0:T(8,128)(2,1)} %hidden_hbm.1, f32[1,4096]{1,0:T(1,128)} %bitcast.56), custom_call_target="tpu_custom_call" | custom-call | tf_op jit(solution)/shard_map/norm/pallas_call | solution.py:305
  1.9 4.1 %collective-permute-start.1 = (bf16[24,4096]{1,0:T(8,128)(2,1)S(1)}, bf16[24,4096]{1,0:T(8,128)(2,1)S(1)}, u32[]{:S(2)}, u32[]{:S(2)}) collective-permute-start(bf16[24,4096]{1,0:T(8,128)(2,1)S(1)} %norm.1.refs_2_), channel_id=1, source_target_pairs={{16,0},{9,1},{18,2},{11,3},{20,4},{13,5},{22,6},{15,7},{24,8},{1,9... | collective-permute-start | bytes 589832 | tf_op jit(solution)/shard_map/ppermute | solution.py:246
  6.1 1.5 %collective-permute-start = (bf16[24,4096]{1,0:T(8,128)(2,1)S(1)}, bf16[24,4096]{1,0:T(8,128)(2,1)S(1)}, u32[]{:S(2)}, u32[]{:S(2)}) collective-permute-start(bf16[24,4096]{1,0:T(8,128)(2,1)S(1)} %norm.1.refs_2_), channel_id=1, source_target_pairs={{4,0},{5,1},{6,2},{7,3},{0,4},{1,5},{2,6},{3,7},{12,8},{13,9},{14,... | collective-permute-start | bytes 589832 | tf_op jit(solution)/shard_map/ppermute | solution.py:246
  7.6 3.0 %collective-permute-done.1.refs_4_ = bf16[24,4096]{1,0:T(8,128)(2,1)S(1)} collective-permute-done((bf16[24,4096]{1,0:T(8,128)(2,1)S(1)}, bf16[24,4096]{1,0:T(8,128)(2,1)S(1)}, u32[]{:S(2)}, u32[]{:S(2)}) %collective-permute-start.1) | collective-permute-done | bytes 196640 | tf_op jit(solution)/shard_map/ppermute | solution.py:246
  10.6 1.2 %collective-permute-done.refs_3_ = bf16[24,4096]{1,0:T(8,128)(2,1)S(1)} collective-permute-done((bf16[24,4096]{1,0:T(8,128)(2,1)S(1)}, bf16[24,4096]{1,0:T(8,128)(2,1)S(1)}, u32[]{:S(2)}, u32[]{:S(2)}) %collective-permute-start) | collective-permute-done | bytes 196640 | tf_op jit(solution)/shard_map/ppermute | solution.py:246
  11.8 1.6 %collective-permute-start.3 = (bf16[24,4096]{1,0:T(8,128)(2,1)S(1)}, bf16[24,4096]{1,0:T(8,128)(2,1)S(1)}, u32[]{:S(2)}, u32[]{:S(2)}) collective-permute-start(bf16[24,4096]{1,0:T(8,128)(2,1)S(1)} %broadcast_select_fusion), channel_id=1, source_target_pairs={{8,0},{25,1},{10,2},{27,3},{12,4},{29,5},{14,6},{31,7},{0,8},{17,9... | collective-permute-start | bytes 589832 | tf_op jit(solution)/shard_map/ppermute | solution.py:246
  13.4 1.5 %collective-permute-start.2 = (bf16[24,4096]{1,0:T(8,128)(2,1)S(1)}, bf16[24,4096]{1,0:T(8,128)(2,1)S(1)}, u32[]{:S(2)}, u32[]{:S(2)}) collective-permute-start(bf16[24,4096]{1,0:T(8,128)(2,1)S(1)} %collective-permute-done.1.refs_4_), channel_id=1, source_target_pairs={{4,0},{5,1},{6,2},{7,3},{0,4},{1,5},{2,6},{3,7},{12,8},{13,9},{14,... | collective-permute-start | bytes 589832 | tf_op jit(solution)/shard_map/ppermute | solution.py:246
  14.9 4.9 %copy.24 = bf16[512,8,2,256]{3,1,2,0:T(8,128)(2,1)} copy(bf16[512,8,2,256]{3,2,1,0:T(2,128)(2,1)} %bitcast.51) | data formatting | bytes 8388608
  20.5 0.8 %collective-permute-done.4.refs_7_ = bf16[24,4096]{1,0:T(8,128)(2,1)S(1)} collective-permute-done((bf16[24,4096]{1,0:T(8,128)(2,1)S(1)}, bf16[24,4096]{1,0:T(8,128)(2,1)S(1)}, u32[]{:S(2)}, u32[]{:S(2)}) %collective-permute-start.4) | collective-permute-done | bytes 196640 | tf_op jit(solution)/shard_map/ppermute | solution.py:238
  21.9 3.4 %input.1.refs_5_ = bf16[8,24,512]{2,1,0:T(8,128)(2,1)} custom-call(s32[1]{0:T(128)} %bitcast.2.refs_0_, s32[1]{0:T(128)} %bitcast.3.refs_1_, bf16[24,4096]{1,0:T(8,128)(2,1)S(1)} %norm.1.refs_2_, bf16[24,4096]{1,0:T(8,128)(2,1)S(1)} %collective-permute-done.refs_3_, bf16[24,4096]{1,0:T(8,128)(2,1)S(1)} %collective-permute-done.1.refs_4_, ...), custom_call_target="tpu_custom_call" | custom-call | tf_op jit(solution)/shard_map/input/pallas_call | solution.py:335
  25.2 4.2 %all-to-all-start = ((bf16[8,24,512]{2,1,0:T(8,128)(2,1)}), bf16[8,24,512]{2,1,0:T(8,128)(2,1)S(1)}, u32[]{:S(2)}, u32[]{:S(2)}) async-start(bf16[8,24,512]{2,1,0:T(8,128)(2,1)} %input.1.refs_5_), calls=%async_computation | async-start | bytes 393216 | tf_op jit(solution)/shard_map/all_to_all | solution.py:352
  30.2 1.5 %constant_dynamic-slice_fusion.5.refs_1_ = bf16[32,1024]{1,0:T(8,128)(2,1)} fusion(bf16[32,4096]{1,0:T(8,128)(2,1)} %hidden_hbm.1, s32[]{:T(128)S(6)} %select_n.84), kind=kLoop, calls=%fused_computation.23 | loop fusion | bytes 131076 | tf_op jit(solution)/shard_map/dynamic_slice | solution.py:418
  31.6 2.0 %prefetch.3 = (bf16[32,24]{1,0:T(8,128)(2,1)S(1)}, bf16[24,32]{1,0:T(8,128)(2,1)S(1)}, f32[32,1]{1,0:T(8,128)S(1)}, bf16[3,32,2048]{2,1,0:T(8,128)(2,1)S(1)}, f3...) custom-call(bf16[3,32,2048]{2,1,0:T(8,128)(2,1)} %bitcast.54, ...), custom_call_target="tpu_custom_call" | custom-call | tf_op jit(solution)/shard_map/prefetch/pallas_call | solution.py:321
  33.7 4.1 %all-to-all-done.x_new.z_new = bf16[8,24,512]{2,1,0:T(8,128)(2,1)S(1)} async-done(((bf16[8,24,512]{2,1,0:T(8,128)(2,1)}), bf16[8,24,512]{2,1,0:T(8,128)(2,1)S(1)}, u32[]{:S(2)}, u32[]{:S(2)}) %all-to-all-start) | async-done | bytes 196640 | tf_op jit(solution)/shard_map/all_to_all | solution.py:352
  38.4 1.6 %collective-permute-start.8 = (f32[32,288]{1,0:T(8,128)S(1)}, f32[32,288]{1,0:T(8,128)S(1)}, u32[]{:S(2)}, u32[]{:S(2)}) collective-permute-start(f32[32,288]{1,0:T(8,128)S(1)} %get-tuple-element.40.refs_5_.refs_0_), channel_id=1, source_target_pairs={{0,2},{1,3},{2,0},{3,1},{4,6},{5,7},{6,4},{7,5},{8,10},{9,11},{10,... | collective-permute-start | bytes 110600 | tf_op jit(solution)/shard_map/ppermute | solution.py:238
  40.2 2.6 %prefetch.4 = (bf16[256,2048]{1,0:T(8,128)(2,1)S(1)}, f32[1,2048]{1,0:T(1,128)S(1)}, f32[16,2048]{1,0:T(8,128)S(1)}, f32[1,2048]{1,0:T(1,128)S(1)}, f32[8192,128]{1,0:T(8,128)S(1)}) custom-call(bf16[256,2048]{1,0:T(8,128)(2,1)} %refs_0_.2, f32[1,2048]{1,0:T(1,128)} %bitcast.58, f32[16,2048]{1,0:T(8,128)} %refs_2_.1, f32[1,2048]{1,0:T(1,128)} %bitcast.59, ...), custom_call_target="tpu_custom_call" | custom-call | tf_op jit(solution)/shard_map/prefetch/pallas_call | solution.py:321
  43.7 3.3 %state.1 = (bf16[24,2048]{1,0:T(8,128)(2,1)S(1)}, f32[8192,128]{1,0:T(8,128)}) custom-call(f32[32,288]{1,0:T(8,128)S(1)} %get-tuple-element.40.refs_5_.refs_0_, f32[32,288]{1,0:T(8,128)S(1)} %collective-permute-done.7.refs_1_, f32[32,288]{1,0:T(8,128)S(1)} %collective-permute-done.8.refs_2_, f32[32,288]{1,0:T(8,128)S(1)} %collective-permute-done.9.refs_3_, ...), custom_call_target="tpu_custom_call" | custom-call | tf_op jit(solution)/shard_map/state/pallas_call | solution.py:392
  47.0 1.0 %collective-permute-start.10 = (bf16[24,2048]{1,0:T(8,128)(2,1)S(1)}, bf16[24,2048]{1,0:T(8,128)(2,1)S(1)}, u32[]{:S(2)}, u32[]{:S(2)}) collective-permute-start(bf16[24,2048]{1,0:T(8,128)(2,1)S(1)} %get-tuple-element.50.refs_2_), channel_id=1, source_target_pairs={{0,4},{4,0},{8,12},{12,8},{16,20},{20,16},{24,28},{28,24},{1,5},{5... | collective-permute-start | bytes 294920 | tf_op jit(solution)/shard_map/ppermute | solution.py:238
  48.5 1.6 %collective-permute-start.13 = (bf16[24,2048]{1,0:T(8,128)(2,1)S(1)}, bf16[24,2048]{1,0:T(8,128)(2,1)S(1)}, u32[]{:S(2)}, u32[]{:S(2)}) collective-permute-start(bf16[24,2048]{1,0:T(8,128)(2,1)S(1)} %get-tuple-element.50.refs_2_), channel_id=1, source_target_pairs={{0,16},{4,20},{8,24},{12,28},{16,0},{20,4},{24,8},{28,12},{1,17},{... | collective-permute-start | bytes 294920 | tf_op jit(solution)/shard_map/ppermute | solution.py:238
  50.2 1.6 %prefetch.5 = (bf16[2048,512]{1,0:T(8,128)(2,1)S(1)}, bf16[32,1024]{1,0:T(8,128)(2,1)S(1)}) custom-call(bf16[2048,512]{1,0:T(8,128)(2,1)} %refs_0_.3, bf16[32,1024]{1,0:T(8,128)(2,1)} %constant_dynamic-slice_fusion.5.refs_1_, bf16[24,2048]{1,0:T(8,128)(2,1)S(1)} %get-tuple-element.50.refs_2_), custom_call_target="tpu_custom_call" | custom-call | tf_op jit(solution)/shard_map/prefetch/pallas_call | solution.py:321
  51.8 4.0 %collective-permute-done.13 = bf16[24,2048]{1,0:T(8,128)(2,1)S(1)} collective-permute-done((bf16[24,2048]{1,0:T(8,128)(2,1)S(1)}, bf16[24,2048]{1,0:T(8,128)(2,1)S(1)}, u32[]{:S(2)}, u32[]{:S(2)}) %collective-permute-start.13) | collective-permute-done | bytes 98336 | tf_op jit(solution)/shard_map/ppermute | solution.py:238
  55.8 1.1 %collective-permute-start.14 = (bf16[24,2048]{1,0:T(8,128)(2,1)S(1)}, bf16[24,2048]{1,0:T(8,128)(2,1)S(1)}, u32[]{:S(2)}, u32[]{:S(2)}) collective-permute-start(bf16[24,2048]{1,0:T(8,128)(2,1)S(1)} %collective-permute-done.13), channel_id=1, source_target_pairs={{0,4},{4,0},{8,12},{12,8},{16,20},{20,16},{24,28},{28,24},{1,5},{5... | collective-permute-start | bytes 294920 | tf_op jit(solution)/shard_map/ppermute | solution.py:238
  56.9 0.9 %collective-permute-start.12 = (bf16[24,2048]{1,0:T(8,128)(2,1)S(1)}, bf16[24,2048]{1,0:T(8,128)(2,1)S(1)}, u32[]{:S(2)}, u32[]{:S(2)}) collective-permute-start(bf16[24,2048]{1,0:T(8,128)(2,1)S(1)} %collective-permute-done.11), channel_id=1, source_target_pairs={{0,4},{4,0},{8,12},{12,8},{16,20},{20,16},{24,28},{28,24},{1,5},{5... | collective-permute-start | bytes 294920 | tf_op jit(solution)/shard_map/ppermute | solution.py:238
  57.8 1.9 %collective-permute-start.16 = (bf16[24,2048]{1,0:T(8,128)(2,1)S(1)}, bf16[24,2048]{1,0:T(8,128)(2,1)S(1)}, u32[]{:S(2)}, u32[]{:S(2)}) collective-permute-start(bf16[24,2048]{1,0:T(8,128)(2,1)S(1)} %collective-permute-done.10), channel_id=1, source_target_pairs={{0,24},{4,28},{8,16},{12,20},{16,8},{20,12},{24,0},{28,4},{1,25},{... | collective-permute-start | bytes 294920 | tf_op jit(solution)/shard_map/ppermute | solution.py:238
  59.7 1.8 %collective-permute-done.12 = bf16[24,2048]{1,0:T(8,128)(2,1)S(1)} collective-permute-done((bf16[24,2048]{1,0:T(8,128)(2,1)S(1)}, bf16[24,2048]{1,0:T(8,128)(2,1)S(1)}, u32[]{:S(2)}, u32[]{:S(2)}) %collective-permute-start.12) | collective-permute-done | bytes 98336 | tf_op jit(solution)/shard_map/ppermute | solution.py:238
  62.0 2.3 %collective-permute-done.16 = bf16[24,2048]{1,0:T(8,128)(2,1)S(1)} collective-permute-done((bf16[24,2048]{1,0:T(8,128)(2,1)S(1)}, bf16[24,2048]{1,0:T(8,128)(2,1)S(1)}, u32[]{:S(2)}, u32[]{:S(2)}) %collective-permute-start.16) | collective-permute-done | bytes 98336 | tf_op jit(solution)/shard_map/ppermute | solution.py:238
  65.0 1.2 %collective-permute-start.18 = (bf16[48,512]{1,0:T(8,128)(2,1)S(1)}, bf16[48,512]{1,0:T(8,128)(2,1)S(1)}, u32[]{:S(2)}, u32[]{:S(2)}) collective-permute-start(bf16[48,512]{1,0:T(8,128)(2,1)S(1)} %get-tuple-element.57), channel_id=1, source_target_pairs={{0,2},{1,3},{2,0},{3,1},{4,6},{5,7},{6,4},{7,5},{8,10},{9,11},{10,... | collective-permute-start | bytes 147464 | tf_op jit(solution)/shard_map/ppermute | solution.py:238
  67.0 2.1 %collective-permute-done.18 = bf16[48,512]{1,0:T(8,128)(2,1)S(1)} collective-permute-done((bf16[48,512]{1,0:T(8,128)(2,1)S(1)}, bf16[48,512]{1,0:T(8,128)(2,1)S(1)}, u32[]{:S(2)}, u32[]{:S(2)}) %collective-permute-start.18) | collective-permute-done | bytes 49184 | tf_op jit(solution)/shard_map/ppermute | solution.py:238
  70.0 1.4 %collective-permute-start.20 = (bf16[24,512]{1,0:T(8,128)(2,1)S(1)}, bf16[24,512]{1,0:T(8,128)(2,1)S(1)}, u32[]{:S(2)}, u32[]{:S(2)}) collective-permute-start(bf16[24,512]{1,0:T(8,128)(2,1)S(1)} %get-tuple-element.61), channel_id=1, source_target_pairs={{0,16},{1,24},{2,0},{3,8},{4,20},{5,28},{6,4},{7,12},{8,17},{9,25}... | collective-permute-start | bytes 73736 | tf_op jit(solution)/shard_map/ppermute | solution.py:442
  71.4 1.8 %collective-permute-start.21 = (bf16[24,512]{1,0:T(8,128)(2,1)S(1)}, bf16[24,512]{1,0:T(8,128)(2,1)S(1)}, u32[]{:S(2)}, u32[]{:S(2)}) collective-permute-start(bf16[24,512]{1,0:T(8,128)(2,1)S(1)} %get-tuple-element.60), channel_id=1, source_target_pairs={{0,20},{1,28},{2,4},{3,12},{4,16},{5,24},{6,0},{7,8},{8,21},{9,29}... | collective-permute-start | bytes 73736 | tf_op jit(solution)/shard_map/ppermute | solution.py:442
  73.2 0.9 %fusion = bf16[32,3,2048]{2,0,1:T(8,128)(2,1)} fusion(bf16[1,32,2048]{2,1,0:T(8,128)(2,1)S(1)} %bitcast.48, bf16[2,32,2048]{2,1,0:T(8,128)(2,1)S(1)} %slice.4, pred[32]{0:T(512)(128)(4,1)S(1)} %fusion.2, bf16[32,3,2048]{2,0,1:T(8,128)(2,1)S(1)} %copy-done.1), kind=kLoop, calls=%fused_computation.2 | loop fusion | flops 393216 | bytes 1179680 | tf_op jit(solution)/shard_map/transpose | solution.py:417
  74.1 2.0 %collective-permute-done.21 = bf16[24,512]{1,0:T(8,128)(2,1)S(1)} collective-permute-done((bf16[24,512]{1,0:T(8,128)(2,1)S(1)}, bf16[24,512]{1,0:T(8,128)(2,1)S(1)}, u32[]{:S(2)}, u32[]{:S(2)}) %collective-permute-start.21) | collective-permute-done | bytes 24608 | tf_op jit(solution)/shard_map/ppermute | solution.py:442
  (50 shorter events, 6.9 us)
Async XLA Ops:
  1.9 8.6 %collective-permute-start.1 = (bf16[24,4096]{1,0:T(8,128)(2,1)S(1)}, bf16[24,4096]{1,0:T(8,128)(2,1)S(1)}, u32[]{:S(2)}, u32[]{:S(2)}) collective-permute-start(bf16[24,4096]{1,0:T(8,128)(2,1)S(1)} %norm.1.refs_2_), channel_id=1, source_target_pairs={{16,0},{9,1},{18,2},{11,3},{20,4},{13,5},{22,6},{15,7},{24,8},{1,9... | collective-permute-start | bytes 589832 | tf_op jit(solution)/shard_map/ppermute | solution.py:246
  6.1 5.7 %collective-permute-start = (bf16[24,4096]{1,0:T(8,128)(2,1)S(1)}, bf16[24,4096]{1,0:T(8,128)(2,1)S(1)}, u32[]{:S(2)}, u32[]{:S(2)}) collective-permute-start(bf16[24,4096]{1,0:T(8,128)(2,1)S(1)} %norm.1.refs_2_), channel_id=1, source_target_pairs={{4,0},{5,1},{6,2},{7,3},{0,4},{1,5},{2,6},{3,7},{12,8},{13,9},{14,... | collective-permute-start | bytes 589832 | tf_op jit(solution)/shard_map/ppermute | solution.py:246
  11.8 8.1 %collective-permute-start.3 = (bf16[24,4096]{1,0:T(8,128)(2,1)S(1)}, bf16[24,4096]{1,0:T(8,128)(2,1)S(1)}, u32[]{:S(2)}, u32[]{:S(2)}) collective-permute-start(bf16[24,4096]{1,0:T(8,128)(2,1)S(1)} %broadcast_select_fusion), channel_id=1, source_target_pairs={{8,0},{25,1},{10,2},{27,3},{12,4},{29,5},{14,6},{31,7},{0,8},{17,9... | collective-permute-start | bytes 589832 | tf_op jit(solution)/shard_map/ppermute | solution.py:246
  13.4 6.5 %collective-permute-start.2 = (bf16[24,4096]{1,0:T(8,128)(2,1)S(1)}, bf16[24,4096]{1,0:T(8,128)(2,1)S(1)}, u32[]{:S(2)}, u32[]{:S(2)}) collective-permute-start(bf16[24,4096]{1,0:T(8,128)(2,1)S(1)} %collective-permute-done.1.refs_4_), channel_id=1, source_target_pairs={{4,0},{5,1},{6,2},{7,3},{0,4},{1,5},{2,6},{3,7},{12,8},{13,9},{14,... | collective-permute-start | bytes 589832 | tf_op jit(solution)/shard_map/ppermute | solution.py:246
  19.9 10.2 %copy-start.2 = (s32[32]{0:T(128)S(1)}, s32[32]{0:T(128)}, u32[]{:S(2)}) copy-start(s32[32]{0:T(128)} %param.31) | copy-start | bytes 388
  19.9 11.8 %copy-start = (s32[1,32]{1,0:T(1,128)S(1)}, s32[1,32]{1,0:T(1,128)}, u32[]{:S(2)}) copy-start(s32[1,32]{1,0:T(1,128)} %refs_6_.1) | copy-start | bytes 388
  19.9 1.4 %collective-permute-start.4 = (bf16[24,4096]{1,0:T(8,128)(2,1)S(1)}, bf16[24,4096]{1,0:T(8,128)(2,1)S(1)}, u32[]{:S(2)}, u32[]{:S(2)}) collective-permute-start(bf16[24,4096]{1,0:T(8,128)(2,1)S(1)} %collective-permute-done.1.refs_4_), channel_id=1, source_target_pairs={{0,1},{1,0},{2,3},{3,2},{4,5},{5,4},{6,7},{7,6},{8,9},{9,8},{10,11... | collective-permute-start | bytes 589832 | tf_op jit(solution)/shard_map/ppermute | solution.py:238
  19.9 1.7 %collective-permute-start.5 = (bf16[24,4096]{1,0:T(8,128)(2,1)S(1)}, bf16[24,4096]{1,0:T(8,128)(2,1)S(1)}, u32[]{:S(2)}, u32[]{:S(2)}) collective-permute-start(bf16[24,4096]{1,0:T(8,128)(2,1)S(1)} %collective-permute-done.2.refs_5_), channel_id=1, source_target_pairs={{0,1},{1,0},{2,3},{3,2},{4,5},{5,4},{6,7},{7,6},{8,9},{9,8},{10,11... | collective-permute-start | bytes 589832 | tf_op jit(solution)/shard_map/ppermute | solution.py:238
  20.4 1.5 %collective-permute-start.6 = (bf16[24,4096]{1,0:T(8,128)(2,1)S(1)}, bf16[24,4096]{1,0:T(8,128)(2,1)S(1)}, u32[]{:S(2)}, u32[]{:S(2)}) collective-permute-start(bf16[24,4096]{1,0:T(8,128)(2,1)S(1)} %collective-permute-done.3.refs_6_), channel_id=1, source_target_pairs={{0,1},{1,0},{2,3},{3,2},{4,5},{5,4},{6,7},{7,6},{8,9},{9,8},{10,11... | collective-permute-start | bytes 589832 | tf_op jit(solution)/shard_map/ppermute | solution.py:238
  25.2 12.5 %all-to-all-start = ((bf16[8,24,512]{2,1,0:T(8,128)(2,1)}), bf16[8,24,512]{2,1,0:T(8,128)(2,1)S(1)}, u32[]{:S(2)}, u32[]{:S(2)}) async-start(bf16[8,24,512]{2,1,0:T(8,128)(2,1)} %input.1.refs_5_), calls=%async_computation | async-start | bytes 393216 | tf_op jit(solution)/shard_map/all_to_all | solution.py:352
  38.3 4.6 %collective-permute-start.7 = (f32[32,288]{1,0:T(8,128)S(1)}, f32[32,288]{1,0:T(8,128)S(1)}, u32[]{:S(2)}, u32[]{:S(2)}) collective-permute-start(f32[32,288]{1,0:T(8,128)S(1)} %get-tuple-element.40.refs_5_.refs_0_), channel_id=1, source_target_pairs={{0,1},{1,0},{2,3},{3,2},{4,5},{5,4},{6,7},{7,6},{8,9},{9,8},{10,11... | collective-permute-start | bytes 110600 | tf_op jit(solution)/shard_map/ppermute | solution.py:238
  38.4 4.5 %collective-permute-start.8 = (f32[32,288]{1,0:T(8,128)S(1)}, f32[32,288]{1,0:T(8,128)S(1)}, u32[]{:S(2)}, u32[]{:S(2)}) collective-permute-start(f32[32,288]{1,0:T(8,128)S(1)} %get-tuple-element.40.refs_5_.refs_0_), channel_id=1, source_target_pairs={{0,2},{1,3},{2,0},{3,1},{4,6},{5,7},{6,4},{7,5},{8,10},{9,11},{10,... | collective-permute-start | bytes 110600 | tf_op jit(solution)/shard_map/ppermute | solution.py:238
  39.9 3.7 %collective-permute-start.9 = (f32[32,288]{1,0:T(8,128)S(1)}, f32[32,288]{1,0:T(8,128)S(1)}, u32[]{:S(2)}, u32[]{:S(2)}) collective-permute-start(f32[32,288]{1,0:T(8,128)S(1)} %get-tuple-element.40.refs_5_.refs_0_), channel_id=1, source_target_pairs={{0,3},{1,2},{2,1},{3,0},{4,7},{5,6},{6,5},{7,4},{8,11},{9,10},{10,... | collective-permute-start | bytes 110600 | tf_op jit(solution)/shard_map/ppermute | solution.py:238
  47.0 20.0 %copy-start.1 = (bf16[32,3,2048]{2,0,1:T(8,128)(2,1)S(1)}, bf16[32,3,2048]{2,0,1:T(8,128)(2,1)}, u32[]{:S(2)}) copy-start(bf16[32,3,2048]{2,0,1:T(8,128)(2,1)} %param.29) | copy-start | bytes 1179652
  47.0 10.8 %collective-permute-start.10 = (bf16[24,2048]{1,0:T(8,128)(2,1)S(1)}, bf16[24,2048]{1,0:T(8,128)(2,1)S(1)}, u32[]{:S(2)}, u32[]{:S(2)}) collective-permute-start(bf16[24,2048]{1,0:T(8,128)(2,1)S(1)} %get-tuple-element.50.refs_2_), channel_id=1, source_target_pairs={{0,4},{4,0},{8,12},{12,8},{16,20},{20,16},{24,28},{28,24},{1,5},{5... | collective-permute-start | bytes 294920 | tf_op jit(solution)/shard_map/ppermute | solution.py:238
  48.0 8.8 %collective-permute-start.11 = (bf16[24,2048]{1,0:T(8,128)(2,1)S(1)}, bf16[24,2048]{1,0:T(8,128)(2,1)S(1)}, u32[]{:S(2)}, u32[]{:S(2)}) collective-permute-start(bf16[24,2048]{1,0:T(8,128)(2,1)S(1)} %get-tuple-element.50.refs_2_), channel_id=1, source_target_pairs={{0,8},{4,12},{8,0},{12,4},{16,24},{20,28},{24,16},{28,20},{1,9},{5... | collective-permute-start | bytes 294920 | tf_op jit(solution)/shard_map/ppermute | solution.py:238
  48.5 7.3 %collective-permute-start.13 = (bf16[24,2048]{1,0:T(8,128)(2,1)S(1)}, bf16[24,2048]{1,0:T(8,128)(2,1)S(1)}, u32[]{:S(2)}, u32[]{:S(2)}) collective-permute-start(bf16[24,2048]{1,0:T(8,128)(2,1)S(1)} %get-tuple-element.50.refs_2_), channel_id=1, source_target_pairs={{0,16},{4,20},{8,24},{12,28},{16,0},{20,4},{24,8},{28,12},{1,17},{... | collective-permute-start | bytes 294920 | tf_op jit(solution)/shard_map/ppermute | solution.py:238
  55.8 5.8 %collective-permute-start.14 = (bf16[24,2048]{1,0:T(8,128)(2,1)S(1)}, bf16[24,2048]{1,0:T(8,128)(2,1)S(1)}, u32[]{:S(2)}, u32[]{:S(2)}) collective-permute-start(bf16[24,2048]{1,0:T(8,128)(2,1)S(1)} %collective-permute-done.13), channel_id=1, source_target_pairs={{0,4},{4,0},{8,12},{12,8},{16,20},{20,16},{24,28},{28,24},{1,5},{5... | collective-permute-start | bytes 294920 | tf_op jit(solution)/shard_map/ppermute | solution.py:238
  56.9 5.1 %collective-permute-start.15 = (bf16[24,2048]{1,0:T(8,128)(2,1)S(1)}, bf16[24,2048]{1,0:T(8,128)(2,1)S(1)}, u32[]{:S(2)}, u32[]{:S(2)}) collective-permute-start(bf16[24,2048]{1,0:T(8,128)(2,1)S(1)} %collective-permute-done.13), channel_id=1, source_target_pairs={{0,8},{4,12},{8,0},{12,4},{16,24},{20,28},{24,16},{28,20},{1,9},{5... | collective-permute-start | bytes 294920 | tf_op jit(solution)/shard_map/ppermute | solution.py:238
  56.9 4.6 %collective-permute-start.12 = (bf16[24,2048]{1,0:T(8,128)(2,1)S(1)}, bf16[24,2048]{1,0:T(8,128)(2,1)S(1)}, u32[]{:S(2)}, u32[]{:S(2)}) collective-permute-start(bf16[24,2048]{1,0:T(8,128)(2,1)S(1)} %collective-permute-done.11), channel_id=1, source_target_pairs={{0,4},{4,0},{8,12},{12,8},{16,20},{20,16},{24,28},{28,24},{1,5},{5... | collective-permute-start | bytes 294920 | tf_op jit(solution)/shard_map/ppermute | solution.py:238
  57.8 6.5 %collective-permute-start.16 = (bf16[24,2048]{1,0:T(8,128)(2,1)S(1)}, bf16[24,2048]{1,0:T(8,128)(2,1)S(1)}, u32[]{:S(2)}, u32[]{:S(2)}) collective-permute-start(bf16[24,2048]{1,0:T(8,128)(2,1)S(1)} %collective-permute-done.10), channel_id=1, source_target_pairs={{0,24},{4,28},{8,16},{12,20},{16,8},{20,12},{24,0},{28,4},{1,25},{... | collective-permute-start | bytes 294920 | tf_op jit(solution)/shard_map/ppermute | solution.py:238
  64.9 2.1 %collective-permute-start.17 = (bf16[48,512]{1,0:T(8,128)(2,1)S(1)}, bf16[48,512]{1,0:T(8,128)(2,1)S(1)}, u32[]{:S(2)}, u32[]{:S(2)}) collective-permute-start(bf16[48,512]{1,0:T(8,128)(2,1)S(1)} %get-tuple-element.55), channel_id=1, source_target_pairs={{0,1},{1,0},{2,3},{3,2},{4,5},{5,4},{6,7},{7,6},{8,9},{9,8},{10,11... | collective-permute-start | bytes 147464 | tf_op jit(solution)/shard_map/ppermute | solution.py:238
  65.0 4.2 %collective-permute-start.18 = (bf16[48,512]{1,0:T(8,128)(2,1)S(1)}, bf16[48,512]{1,0:T(8,128)(2,1)S(1)}, u32[]{:S(2)}, u32[]{:S(2)}) collective-permute-start(bf16[48,512]{1,0:T(8,128)(2,1)S(1)} %get-tuple-element.57), channel_id=1, source_target_pairs={{0,2},{1,3},{2,0},{3,1},{4,6},{5,7},{6,4},{7,5},{8,10},{9,11},{10,... | collective-permute-start | bytes 147464 | tf_op jit(solution)/shard_map/ppermute | solution.py:238
  66.2 3.7 %collective-permute-start.19 = (bf16[48,512]{1,0:T(8,128)(2,1)S(1)}, bf16[48,512]{1,0:T(8,128)(2,1)S(1)}, u32[]{:S(2)}, u32[]{:S(2)}) collective-permute-start(bf16[48,512]{1,0:T(8,128)(2,1)S(1)} %get-tuple-element.56), channel_id=1, source_target_pairs={{0,3},{1,2},{2,1},{3,0},{4,7},{5,6},{6,5},{7,4},{8,11},{9,10},{10,... | collective-permute-start | bytes 147464 | tf_op jit(solution)/shard_map/ppermute | solution.py:238
  70.0 4.1 %collective-permute-start.20 = (bf16[24,512]{1,0:T(8,128)(2,1)S(1)}, bf16[24,512]{1,0:T(8,128)(2,1)S(1)}, u32[]{:S(2)}, u32[]{:S(2)}) collective-permute-start(bf16[24,512]{1,0:T(8,128)(2,1)S(1)} %get-tuple-element.61), channel_id=1, source_target_pairs={{0,16},{1,24},{2,0},{3,8},{4,20},{5,28},{6,4},{7,12},{8,17},{9,25}... | collective-permute-start | bytes 73736 | tf_op jit(solution)/shard_map/ppermute | solution.py:442
  71.4 4.7 %collective-permute-start.21 = (bf16[24,512]{1,0:T(8,128)(2,1)S(1)}, bf16[24,512]{1,0:T(8,128)(2,1)S(1)}, u32[]{:S(2)}, u32[]{:S(2)}) collective-permute-start(bf16[24,512]{1,0:T(8,128)(2,1)S(1)} %get-tuple-element.60), channel_id=1, source_target_pairs={{0,20},{1,28},{2,4},{3,12},{4,16},{5,24},{6,0},{7,8},{8,21},{9,29}... | collective-permute-start | bytes 73736 | tf_op jit(solution)/shard_map/ppermute | solution.py:442
where the time goes:
time: 77.9 us; the launch traced here: 76.9 us
  starting transfers between devices  27.6 us (35%)
  waiting for transfers between devices  23.9 us (31%)
  Pallas kernels  15.5 us (20%)
  local copies, waits for them, and re-layouts  6.73 us (9%)
  between operations  1.57 us (2%)
  other arithmetic  1.02 us (1%)
    ppermute x16, waiting for transfers between devices, swap_by(): return lax.ppermute(values, axis, [(i, i ^ mask) for i in range(size)])  13.5 us
    ppermute x16, starting transfers between devices, swap_by(): return lax.ppermute(values, axis, [(i, i ^ mask) for i in range(size)])  11.4 us
    ppermute x4, starting transfers between devices, swap_by_core(): return lax.ppermute(values, ('dp', 'tensor'), perm)  8.81 us
    pallas_call x3, Pallas kernels, prefetch(): pl.pallas_call(lambda *refs: prefetch_kernel(*refs, parts=len(values)), o...  6.24 us
    unnamed x7, local copies, waits for them, and re-layouts  4.95 us
    all_to_all x1, starting transfers between devices, body(): lax.all_to_all(branches, 'dp', split_axis=0, concat_axis=0, tiled=True)  4.18 us
    ppermute x4, waiting for transfers between devices, swap_by_core(): return lax.ppermute(values, ('dp', 'tensor'), perm)  4.15 us
    all_to_all x1, waiting for transfers between devices, body(): lax.all_to_all(branches, 'dp', split_axis=0, concat_axis=0, tiled=True)  4.13 us
  transfers between devices with their start and end apart: 23, of which 14 were waited for; matrix products, arithmetic and copies ran while one was open for 10% of the time, Pallas kernels for 8%

commit v1 on v0

--- a/solution.py
+++ b/solution.py
@@ -78,12 +78,24 @@
     return one_hot
 
 
+def row_pieces(shape, dtype):
+    size = jnp.dtype(dtype).itemsize
+    for extent in shape:
+        size *= extent
+    cuts = 1
+    while size // cuts > 2**18 and shape[0] % (32 * cuts) == 0:
+        cuts *= 2
+    rows = shape[0] // cuts
+    return [pl.ds(i * rows, rows) for i in range(cuts)]
+
+
 def prefetch_kernel(*refs, parts):
     sources, targets, sems = refs[:parts], refs[parts + 1 :][-parts - 1 : -1], refs[-1]
     extra = refs[parts + 1 : -parts - 1]
-    copies = [
-        pltpu.make_async_copy(a, b, sems.at[i]) for i, (a, b) in enumerate(zip(sources, targets))
-    ]
+    copies = []
+    for a, b in zip(sources, targets):
+        for at in row_pieces(a.shape, a.dtype):
+            copies.append(pltpu.make_async_copy(a.at[at], b.at[at], sems.at[len(copies)]))
     for copy in copies:
         copy.start()
     if extra:
@@ -96,27 +108,26 @@
         copy.wait()
 
 
+def flush_kernel(source, target, sems):
+    copies = [
+        pltpu.make_async_copy(source.at[at], target.at[at], sems.at[i])
+        for i, at in enumerate(row_pieces(source.shape, source.dtype))
+    ]
+    for copy in copies:
+        copy.start()
+    for copy in copies:
+        copy.wait()
+
+
 def input_kernel(*refs, parts):
     own, place = refs[0][0], refs[1][0]
     blocks = refs[2 : 2 + parts]
-    weights_hbm, branches, stacked, weights, sems = refs[2 + parts :]
+    upper, lower, branches, stacked = refs[2 + parts :]
     rows = blocks[0].shape[0]
-    chunks = sems.shape[0]
-    deep = weights.shape[0] // chunks
-    pieces = [slice(i * deep, (i + 1) * deep) for i in range(chunks)]
-    copies = [
-        pltpu.make_async_copy(weights_hbm.at[at, :], weights.at[at, :], sems.at[i])
-        for i, at in enumerate(pieces)
-    ]
-    for copy in copies:
-        copy.start()
     for k, ref in enumerate(blocks):
         stacked[k * rows : (k + 1) * rows, :] = ref[...]
-    result = None
-    for copy, at in zip(copies, pieces):
-        copy.wait()
-        part = jnp.dot(stacked[:, at], weights[at, :], preferred_element_type=F32)
-        result = part if result is None else result + part
+    weights = jnp.concatenate([upper[...], lower[...]], axis=0)
+    result = jnp.dot(stacked[...], weights, preferred_element_type=F32)
     for k in range(parts):
         mask = jnp.where(place % 2 == 0, *SHARED_MASKS[k])
         branches[own ^ mask] = result[k * rows : (k + 1) * rows, :].astype(BF16)
@@ -156,19 +167,13 @@
 def state_kernel(*refs, parts, group, wide):
     sums = refs[:parts]
     (pick, live, w_dt, dt_bias, a_log, d_skip, filtered, z_in, lengths, states,
-     gated, states_next,
-     result, step, drive, b_wide, c_wide, decay, pieces, out_sem) = refs[parts:]
+     gated, result,
+     step, drive, b_wide, c_wide, decay, pieces) = refs[parts:]
     count = a_log.shape[0]
     slots, width = filtered.shape
     chunks = slots // group
     tiles = width // 128
     halves = count // 8
-    span = group * halves * tiles * 8
-
-    def save(k):
-        piece = pl.ds(k * span, span)
-        return pltpu.make_async_copy(result.at[piece], states_next.at[piece], out_sem.at[k])
-
     active = live[...] > 0.5
     total = sums[0][...]
     for other in sums[1:]:
@@ -210,7 +215,6 @@
             return carry
 
         lax.fori_loop(0, tiles // wide, column, 0)
-        save(k).start()
     outputs = []
     for tile in range(tiles):
         y = pieces[pl.ds(tile * slots * 8, slots, stride=8), :]
@@ -221,8 +225,6 @@
     mixed = jnp.concatenate(outputs, axis=1) + d_skip[...] * filt
     mixed = (mixed * silu(z_in[...].astype(F32))).astype(BF16)
     gated[...] = jnp.dot(pick[...], mixed, preferred_element_type=F32).astype(BF16)
-    for k in range(chunks):
-        save(k).wait()
 
 
 def mix_kernel(spread, columns, first, second, mixed):
@@ -249,21 +251,30 @@
 SHARED_MASKS = ((0, 0), (1, 1), (4, 2), (5, 3), (6, 7), (2, 4), (3, 5), (7, 6))
 
 
-def gather_shared(block, weights, t, n_dp, n_t):
+def gather_shared(block, weights, fetch, t, n_dp, n_t):
     even = t % 2 == 0
+    deep = weights.shape[0] // 2
+    block, weights = lax.optimization_barrier((block, weights))
+    upper = weights[:deep].reshape(deep, -1)
     side = swap_by_core(block, n_dp, n_t, (1, 1))
     far = swap_by_core(block, n_dp, n_t, (4, 2))
+    far, upper, weights = lax.optimization_barrier((far, upper, weights))
+    lower = weights[deep:].reshape(deep, -1)
     far_side = swap_by_core(far, n_dp, n_t, (1, 1))
     last = swap_by_core(jnp.where(even, far, side), n_dp, n_t, (2, 6))
-    weights, far = lax.optimization_barrier((weights, far))
-    weights = weights.reshape(weights.shape[0], -1)
-    weights, far_side, last = lax.optimization_barrier((weights, far_side, last))
+    upper, lower = lax.optimization_barrier((upper, lower))
+    upper, lower, far_side, last = lax.optimization_barrier(
+        (fetch(upper), lower, far_side, last)
+    )
+    lower = fetch(lower)
     swapped = [swap_by(v, "tensor", n_t, 1) for v in (far, far_side, last)]
-    return weights, [block, side, far, far_side, last] + swapped
+    return [upper, lower], [block, side, far, far_side, last] + swapped
 
 
 def gather_own(block, g, n_dp):
-    far, near, side = (swap_by(block, "dp", n_dp, m) for m in (4, 2, 1))
+    near, side = (swap_by(block, "dp", n_dp, m) for m in (2, 1))
+    far = swap_by(block, "dp", n_dp, 4)
+    side, far = lax.optimization_barrier((side, far))
     both = swap_by(far, "dp", n_dp, 2)
     near_side = swap_by(near, "dp", n_dp, 1)
     far_side = swap_by(far, "dp", n_dp, 1)
@@ -325,26 +336,31 @@
                 + [pl.BlockSpec(memory_space=pl.ANY)]
                 + [SMEM] * (2 if matrices else 0),
                 out_specs=(VMEM,) * (len(values) + len(matrices)),
-                scratch_shapes=[pltpu.SemaphoreType.DMA((len(values),))],
+                scratch_shapes=[
+                    pltpu.SemaphoreType.DMA(
+                        (sum(len(row_pieces(v.shape, v.dtype)) for v in values),)
+                    )
+                ],
                 compiler_params=limit(1),
                 name="prefetch",
             )(*[away(v) for v in values], after, *((ids, held) if matrices else ()))
 
         if direct:
-            weights, blocks = gather_shared(chosen, w_in, t, n_dp, n_t)
+            def fetch(values):
+                return prefetch((values,), chosen)[0]
+
+            weights, blocks = gather_shared(chosen, w_in, fetch, t, n_dp, n_t)
             branches = pl.pallas_call(
                 lambda *refs: input_kernel(*refs, parts=n_dp),
                 out_shape=out((n_dp, rows, 2 * block), BF16),
-                in_specs=[SMEM] * 2 + [VMEM] * n_dp + [HBM],
+                in_specs=[SMEM] * 2 + [VMEM] * (n_dp + 2),
                 out_specs=VMEM,
                 scratch_shapes=[
                     pltpu.VMEM((n_dp * rows, depth), BF16),
-                    pltpu.VMEM(weights.shape, BF16),
-                    pltpu.SemaphoreType.DMA((4,)),
                 ],
                 compiler_params=limit(12),
                 name="input",
-            )(own, place, *[near(b) for b in blocks], away(weights))
+            )(own, place, *[near(b) for b in blocks], *[near(w) for w in weights])
         else:
             full = lax.all_gather(chosen, "dp", axis=0, tiled=True)
             branches = jnp.dot(full, w_in.reshape(depth, 2 * block), preferred_element_type=F32)
@@ -391,23 +407,30 @@
         group, wide = 8, 2
         gated, states_next = pl.pallas_call(
             lambda *refs: state_kernel(*refs, parts=len(sums), group=group, wide=wide),
-            out_shape=(near_out((rows, width), BF16), out((flat, 128), F32)),
+            out_shape=(near_out((rows, width), BF16), near_out((flat, 128), F32)),
             in_specs=[VMEM] * (len(sums) + 10),
-            out_specs=(VMEM, HBM),
+            out_specs=(VMEM, VMEM),
             scratch_shapes=[
-                pltpu.VMEM((flat, 128), F32),
                 pltpu.VMEM((slots, width), F32),
                 pltpu.VMEM((slots, width), F32),
                 pltpu.VMEM((slots * count, 128), F32),
                 pltpu.VMEM((slots * count, 128), F32),
                 pltpu.VMEM((count, width), F32),
                 pltpu.VMEM((slots * width // 16, 128), F32),
-                pltpu.SemaphoreType.DMA((slots // group,)),
             ],
-            compiler_params=limit(12),
+            compiler_params=limit(8),
             name="state",
         )(*[near(v) for v in sums], near(pick), near(live), near(w_dt_n), near(bias_n), near(a_log_n),
           near(skip_n), near(filtered), near(z_in), near(known), near(states_n))
+        states_next = pl.pallas_call(
+            flush_kernel,
+            out_shape=out((flat, 128), F32),
+            in_specs=[VMEM],
+            out_specs=HBM,
+            scratch_shapes=[pltpu.SemaphoreType.DMA((len(row_pieces((flat, 128), F32)),))],
+            compiler_params=limit(1),
+            name="flush",
+        )(near(states_next))
         states_next = states_next.reshape(slots, count // 8, width // 128, 8, 128)
         states_next = jnp.transpose(states_next, (0, 1, 3, 2, 4))
         early = jnp.arange(slots, dtype=jnp.int32) < active_count[0]

time: 77.9 us -> 77.3 us (level)
  waiting for transfers between devices: 23.9 us -> 16.9 us
  Pallas kernels: 15.5 us -> 19.1 us
  local copies, waits for them, and re-layouts: 6.73 us -> 9.33 us
    pallas_call x3 -> x5, Pallas kernels: 6.24 us -> 9.45 us  [prefetch(): pl.pallas_call(lambda *refs: prefetch_kernel(*refs, parts=len(values)), o...]
    ppermute x4, waiting for transfers between devices: 4.15 us -> 1.63 us  [swap_by_core(): return lax.ppermute(values, ('dp', 'tensor'), perm)]
    ppermute x16, waiting for transfers between devices: 13.5 us -> 11.3 us  [swap_by(): return lax.ppermute(values, axis, [(i, i ^ mask) for i in range(size)])]
    pallas_call x0 -> x1, Pallas kernels: none -> 2.13 us  [body(): pl.pallas_call(flush_kernel, out_shape=out((flat, 128), F32), in_specs=[V...]
    ppermute x2, waiting for transfers between devices: 2.04 us -> 0.01 us  [body(): got.append(lax.ppermute(sent, ('dp', 'tensor'), perm))]
    slice x0 -> x4, local copies, waits for them, and re-layouts: none -> 1.6 us  [the longest x2 1.59 us: gather_shared(): upper = weights[:deep].reshape(deep, -1)]
    unnamed x7 -> x12, local copies, waits for them, and re-layouts: 4.95 us -> 5.94 us
    pallas_call x1, Pallas kernels: 3.33 us -> 2.34 us  [body(): pl.pallas_call(lambda *refs: state_kernel(*refs, parts=len(sums), group=g...]
  transfers between devices with their start and end apart: 23 -> 23, of which waited for: 14 -> 10; matrix products, arithmetic and copies ran while one was open for 10% -> 8% of each run, Pallas kernels for 8% -> 15%
where the time goes in v1:
time: 77.3 us; the launch traced here: 76.5 us
  starting transfers between devices  27.9 us (36%)
  Pallas kernels  19.1 us (25%)
  waiting for transfers between devices  16.9 us (22%)
  local copies, waits for them, and re-layouts  9.33 us (12%)
  between operations  1.68 us (2%)
  other arithmetic  1.02 us (1%)
    ppermute x16, waiting for transfers between devices, swap_by(): return lax.ppermute(values, axis, [(i, i ^ mask) for i in range(size)])  11.3 us
    ppermute x16, starting transfers between devices, swap_by(): return lax.ppermute(values, axis, [(i, i ^ mask) for i in range(size)])  10.9 us
    pallas_call x5, Pallas kernels, prefetch(): pl.pallas_call(lambda *refs: prefetch_kernel(*refs, parts=len(values)), o...  9.45 us
    ppermute x4, starting transfers between devices, swap_by_core(): return lax.ppermute(values, ('dp', 'tensor'), perm)  8.81 us
    unnamed x12, local copies, waits for them, and re-layouts  5.94 us
    all_to_all x1, starting transfers between devices, body(): lax.all_to_all(branches, 'dp', split_axis=0, concat_axis=0, tiled=True)  4.89 us
    all_to_all x1, waiting for transfers between devices, body(): lax.all_to_all(branches, 'dp', split_axis=0, concat_axis=0, tiled=True)  3.88 us
    ppermute x2, starting transfers between devices, body(): got.append(lax.ppermute(sent, ('dp', 'tensor'), perm))  3.31 us
  transfers between devices with their start and end apart: 23, of which 10 were waited for; matrix products, arithmetic and copies ran while one was open for 8% of the time, Pallas kernels for 15%

profile of v1, /device:TPU:0, one launch (start us, length us, event | category | flops | bytes accessed | tf_op | source)
XLA Modules:
  0.0 76.5 jit_solution(14624179747499519369)
XLA Ops:
  0.6 1.3 %norm.1.refs_1_.refs_2_ = bf16[24,4096]{1,0:T(8,128)(2,1)S(1)} custom-call(s32[1,32]{1,0:T(1,128)} %refs_6_.1, bf16[32,4096]{1,0:T(8,128)(2,1)} %hidden_hbm.1, f32[1,4096]{1,0:T(1,128)} %bitcast.63), custom_call_target="tpu_custom_call" | custom-call | tf_op jit(solution)/shard_map/norm/pallas_call | solution.py:316
  1.9 4.1 %collective-permute-start.1 = (bf16[24,4096]{1,0:T(8,128)(2,1)S(1)}, bf16[24,4096]{1,0:T(8,128)(2,1)S(1)}, u32[]{:S(2)}, u32[]{:S(2)}) collective-permute-start(bf16[24,4096]{1,0:T(8,128)(2,1)S(1)} %norm.1.refs_1_.refs_2_), channel_id=1, source_target_pairs={{16,0},{9,1},{18,2},{11,3},{20,4},{13,5},{22,6},{15,7},{24,8},{1,9... | collective-permute-start | bytes 589832 | tf_op jit(solution)/shard_map/ppermute | solution.py:248
  6.1 1.5 %collective-permute-start = (bf16[24,4096]{1,0:T(8,128)(2,1)S(1)}, bf16[24,4096]{1,0:T(8,128)(2,1)S(1)}, u32[]{:S(2)}, u32[]{:S(2)}) collective-permute-start(bf16[24,4096]{1,0:T(8,128)(2,1)S(1)} %norm.1.refs_1_.refs_2_), channel_id=1, source_target_pairs={{4,0},{5,1},{6,2},{7,3},{0,4},{1,5},{2,6},{3,7},{12,8},{13,9},{14,... | collective-permute-start | bytes 589832 | tf_op jit(solution)/shard_map/ppermute | solution.py:248
  7.6 1.6 %slice-done = bf16[2048,2,1,256]{3,1,2,0:T(2,128)(2,1)S(1)} async-done(((bf16[4096,2,1,256]{3,1,2,0:T(2,128)(2,1)}), bf16[2048,2,1,256]{3,1,2,0:T(2,128)(2,1)S(1)}, s32[]{:S(2)}) %slice-start) | async-done | bytes 2097176 | tf_op jit(solution)/shard_map/slice | solution.py:258
  9.2 1.8 %copy.24 = bf16[256,8,2,256]{3,1,2,0:T(8,128)(2,1)} copy(bf16[256,8,2,256]{3,2,1,0:T(2,128)(2,1)S(1)} %bitcast.56) | data formatting | bytes 4194304
  11.8 1.6 %collective-permute-start.3 = (bf16[24,4096]{1,0:T(8,128)(2,1)S(1)}, bf16[24,4096]{1,0:T(8,128)(2,1)S(1)}, u32[]{:S(2)}, u32[]{:S(2)}) collective-permute-start(bf16[24,4096]{1,0:T(8,128)(2,1)S(1)} %broadcast_select_fusion), channel_id=1, source_target_pairs={{8,0},{25,1},{10,2},{27,3},{12,4},{29,5},{14,6},{31,7},{0,8},{17,9... | collective-permute-start | bytes 589832 | tf_op jit(solution)/shard_map/ppermute | solution.py:248
  13.4 1.5 %collective-permute-start.2 = (bf16[24,4096]{1,0:T(8,128)(2,1)S(1)}, bf16[24,4096]{1,0:T(8,128)(2,1)S(1)}, u32[]{:S(2)}, u32[]{:S(2)}) collective-permute-start(bf16[24,4096]{1,0:T(8,128)(2,1)S(1)} %collective-permute-done.1.refs_4_), channel_id=1, source_target_pairs={{4,0},{5,1},{6,2},{7,3},{0,4},{1,5},{2,6},{3,7},{12,8},{13,9},{14,... | collective-permute-start | bytes 589832 | tf_op jit(solution)/shard_map/ppermute | solution.py:248
  14.9 1.9 %copy.25 = bf16[256,8,2,256]{3,1,2,0:T(8,128)(2,1)} copy(bf16[256,8,2,256]{3,2,1,0:T(2,128)(2,1)S(1)} %bitcast.57) | data formatting | bytes 4194304
  16.8 1.6 %prefetch.5.refs_10_ = bf16[2048,512]{1,0:T(8,128)(2,1)S(1)} custom-call(bf16[2048,512]{1,0:T(8,128)(2,1)} %bitcast.55, bf16[24,4096]{1,0:T(8,128)(2,1)S(1)} %norm.1.refs_1_.refs_2_), custom_call_target="tpu_custom_call" | custom-call | tf_op jit(solution)/shard_map/prefetch/pallas_call | solution.py:332
  19.8 1.6 %prefetch.6.refs_11_ = bf16[2048,512]{1,0:T(8,128)(2,1)S(1)} custom-call(bf16[2048,512]{1,0:T(8,128)(2,1)} %bitcast.54, bf16[24,4096]{1,0:T(8,128)(2,1)S(1)} %norm.1.refs_1_.refs_2_), custom_call_target="tpu_custom_call" | custom-call | tf_op jit(solution)/shard_map/prefetch/pallas_call | solution.py:332
  21.5 2.6 %input.1.refs_5_ = bf16[8,24,512]{2,1,0:T(8,128)(2,1)} custom-call(s32[1]{0:T(128)} %bitcast.2.refs_0_, s32[1]{0:T(128)} %bitcast.3.refs_1_, bf16[24,4096]{1,0:T(8,128)(2,1)S(1)} %norm.1.refs_1_.refs_2_, bf16[24,4096]{1,0:T(8,128)(2,1)S(1)} %collective-permute-done.refs_3_, bf16[24,4096]{1,0:T(8,128)(2,1)S(1)} %collective-permute-done.1.refs_4_, ...), custom_call_target="tpu_custom_call" | custom-call | tf_op jit(solution)/shard_map/input/pallas_call | solution.py:353
  24.1 4.9 %all-to-all-start = ((bf16[8,24,512]{2,1,0:T(8,128)(2,1)}), bf16[8,24,512]{2,1,0:T(8,128)(2,1)S(1)}, u32[]{:S(2)}, u32[]{:S(2)}) async-start(bf16[8,24,512]{2,1,0:T(8,128)(2,1)} %input.1.refs_5_), calls=%async_computation | async-start | bytes 393216 | tf_op jit(solution)/shard_map/all_to_all | solution.py:368
  29.7 1.5 %constant_dynamic-slice_fusion.5.refs_1_ = bf16[32,1024]{1,0:T(8,128)(2,1)} fusion(bf16[32,4096]{1,0:T(8,128)(2,1)} %hidden_hbm.1, s32[]{:T(128)S(6)} %select_n.84), kind=kLoop, calls=%fused_computation.23 | loop fusion | bytes 131076 | tf_op jit(solution)/shard_map/dynamic_slice | solution.py:441
  31.2 2.0 %prefetch.7 = (bf16[32,24]{1,0:T(8,128)(2,1)S(1)}, bf16[24,32]{1,0:T(8,128)(2,1)S(1)}, f32[32,1]{1,0:T(8,128)S(1)}, bf16[3,32,2048]{2,1,0:T(8,128)(2,1)S(1)}, f3...) custom-call(bf16[3,32,2048]{2,1,0:T(8,128)(2,1)} %bitcast.61, ...), custom_call_target="tpu_custom_call" | custom-call | tf_op jit(solution)/shard_map/prefetch/pallas_call | solution.py:332
  33.2 3.9 %all-to-all-done.x_new.z_new = bf16[8,24,512]{2,1,0:T(8,128)(2,1)S(1)} async-done(((bf16[8,24,512]{2,1,0:T(8,128)(2,1)}), bf16[8,24,512]{2,1,0:T(8,128)(2,1)S(1)}, u32[]{:S(2)}, u32[]{:S(2)}) %all-to-all-start) | async-done | bytes 196640 | tf_op jit(solution)/shard_map/all_to_all | solution.py:368
  37.7 1.6 %collective-permute-start.8 = (f32[32,288]{1,0:T(8,128)S(1)}, f32[32,288]{1,0:T(8,128)S(1)}, u32[]{:S(2)}, u32[]{:S(2)}) collective-permute-start(f32[32,288]{1,0:T(8,128)S(1)} %get-tuple-element.54.refs_5_.refs_0_), channel_id=1, source_target_pairs={{0,2},{1,3},{2,0},{3,1},{4,6},{5,7},{6,4},{7,5},{8,10},{9,11},{10,... | collective-permute-start | bytes 110600 | tf_op jit(solution)/shard_map/ppermute | solution.py:240
  39.5 2.7 %prefetch.8 = (bf16[256,2048]{1,0:T(8,128)(2,1)S(1)}, f32[1,2048]{1,0:T(1,128)S(1)}, f32[16,2048]{1,0:T(8,128)S(1)}, f32[1,2048]{1,0:T(1,128)S(1)}, f32[8192,128]{1,0:T(8,128)S(1)}) custom-call(bf16[256,2048]{1,0:T(8,128)(2,1)} %refs_0_.2, f32[1,2048]{1,0:T(1,128)} %bitcast.65, f32[16,2048]{1,0:T(8,128)} %refs_2_.1, f32[1,2048]{1,0:T(1,128)} %bitcast.66, ...), custom_call_target="tpu_custom_call" | custom-call | tf_op jit(solution)/shard_map/prefetch/pallas_call | solution.py:332
  42.9 2.3 %state.1 = (bf16[24,2048]{1,0:T(8,128)(2,1)S(1)}, f32[8192,128]{1,0:T(8,128)S(1)}) custom-call(f32[32,288]{1,0:T(8,128)S(1)} %get-tuple-element.54.refs_5_.refs_0_, f32[32,288]{1,0:T(8,128)S(1)} %collective-permute-done.7.refs_1_, f32[32,288]{1,0:T(8,128)S(1)} %collective-permute-done.8.refs_2_, f32[32,288]{1,0:T(8,128)S(1)} %collective-permute-done.9.refs_3_, ...), custom_call_target="tpu_custom_call" | custom-call | tf_op jit(solution)/shard_map/state/pallas_call | solution.py:408
  45.3 1.0 %collective-permute-start.10 = (bf16[24,2048]{1,0:T(8,128)(2,1)S(1)}, bf16[24,2048]{1,0:T(8,128)(2,1)S(1)}, u32[]{:S(2)}, u32[]{:S(2)}) collective-permute-start(bf16[24,2048]{1,0:T(8,128)(2,1)S(1)} %get-tuple-element.64.refs_2_), channel_id=1, source_target_pairs={{0,4},{4,0},{8,12},{12,8},{16,20},{20,16},{24,28},{28,24},{1,5},{5... | collective-permute-start | bytes 294920 | tf_op jit(solution)/shard_map/ppermute | solution.py:240
  46.4 2.0 %collective-permute-start.12 = (bf16[24,2048]{1,0:T(8,128)(2,1)S(1)}, bf16[24,2048]{1,0:T(8,128)(2,1)S(1)}, u32[]{:S(2)}, u32[]{:S(2)}) collective-permute-start(bf16[24,2048]{1,0:T(8,128)(2,1)S(1)} %get-tuple-element.64.refs_2_), channel_id=1, source_target_pairs={{0,8},{4,12},{8,0},{12,4},{16,24},{20,28},{24,16},{28,20},{1,9},{5... | collective-permute-start | bytes 294920 | tf_op jit(solution)/shard_map/ppermute | solution.py:240
  48.5 1.6 %prefetch.9 = (bf16[2048,512]{1,0:T(8,128)(2,1)S(1)}, bf16[32,1024]{1,0:T(8,128)(2,1)S(1)}) custom-call(bf16[2048,512]{1,0:T(8,128)(2,1)} %refs_0_.3, bf16[32,1024]{1,0:T(8,128)(2,1)} %constant_dynamic-slice_fusion.5.refs_1_, bf16[24,2048]{1,0:T(8,128)(2,1)S(1)} %get-tuple-element.64.refs_2_), custom_call_target="tpu_custom_call" | custom-call | tf_op jit(solution)/shard_map/prefetch/pallas_call | solution.py:332
  50.2 3.6 %collective-permute-done.11 = bf16[24,2048]{1,0:T(8,128)(2,1)S(1)} collective-permute-done((bf16[24,2048]{1,0:T(8,128)(2,1)S(1)}, bf16[24,2048]{1,0:T(8,128)(2,1)S(1)}, u32[]{:S(2)}, u32[]{:S(2)}) %collective-permute-start.11) | collective-permute-done | bytes 98336 | tf_op jit(solution)/shard_map/ppermute | solution.py:240
  53.8 0.9 %collective-permute-start.14 = (bf16[24,2048]{1,0:T(8,128)(2,1)S(1)}, bf16[24,2048]{1,0:T(8,128)(2,1)S(1)}, u32[]{:S(2)}, u32[]{:S(2)}) collective-permute-start(bf16[24,2048]{1,0:T(8,128)(2,1)S(1)} %collective-permute-done.11), channel_id=1, source_target_pairs={{0,4},{4,0},{8,12},{12,8},{16,20},{20,16},{24,28},{28,24},{1,5},{5... | collective-permute-start | bytes 294920 | tf_op jit(solution)/shard_map/ppermute | solution.py:240
  54.7 1.4 %collective-permute-start.16 = (bf16[24,2048]{1,0:T(8,128)(2,1)S(1)}, bf16[24,2048]{1,0:T(8,128)(2,1)S(1)}, u32[]{:S(2)}, u32[]{:S(2)}) collective-permute-start(bf16[24,2048]{1,0:T(8,128)(2,1)S(1)} %collective-permute-done.10), channel_id=1, source_target_pairs={{0,24},{4,28},{8,16},{12,20},{16,8},{20,12},{24,0},{28,4},{1,25},{... | collective-permute-start | bytes 294920 | tf_op jit(solution)/shard_map/ppermute | solution.py:240
  56.2 1.2 %collective-permute-start.13 = (bf16[24,2048]{1,0:T(8,128)(2,1)S(1)}, bf16[24,2048]{1,0:T(8,128)(2,1)S(1)}, u32[]{:S(2)}, u32[]{:S(2)}) collective-permute-start(bf16[24,2048]{1,0:T(8,128)(2,1)S(1)} %collective-permute-done.12), channel_id=1, source_target_pairs={{0,4},{4,0},{8,12},{12,8},{16,20},{20,16},{24,28},{28,24},{1,5},{5... | collective-permute-start | bytes 294920 | tf_op jit(solution)/shard_map/ppermute | solution.py:240
  57.3 3.5 %collective-permute-done.13 = bf16[24,2048]{1,0:T(8,128)(2,1)S(1)} collective-permute-done((bf16[24,2048]{1,0:T(8,128)(2,1)S(1)}, bf16[24,2048]{1,0:T(8,128)(2,1)S(1)}, u32[]{:S(2)}, u32[]{:S(2)}) %collective-permute-start.13) | collective-permute-done | bytes 98336 | tf_op jit(solution)/shard_map/ppermute | solution.py:240
  62.2 1.0 %collective-permute-start.18 = (bf16[48,512]{1,0:T(8,128)(2,1)S(1)}, bf16[48,512]{1,0:T(8,128)(2,1)S(1)}, u32[]{:S(2)}, u32[]{:S(2)}) collective-permute-start(bf16[48,512]{1,0:T(8,128)(2,1)S(1)} %get-tuple-element.73), channel_id=1, source_target_pairs={{0,2},{1,3},{2,0},{3,1},{4,6},{5,7},{6,4},{7,5},{8,10},{9,11},{10,... | collective-permute-start | bytes 147464 | tf_op jit(solution)/shard_map/ppermute | solution.py:240
  64.2 2.2 %collective-permute-done.18 = bf16[48,512]{1,0:T(8,128)(2,1)S(1)} collective-permute-done((bf16[48,512]{1,0:T(8,128)(2,1)S(1)}, bf16[48,512]{1,0:T(8,128)(2,1)S(1)}, u32[]{:S(2)}, u32[]{:S(2)}) %collective-permute-start.18) | collective-permute-done | bytes 49184 | tf_op jit(solution)/shard_map/ppermute | solution.py:240
  67.2 1.6 %collective-permute-start.20 = (bf16[24,512]{1,0:T(8,128)(2,1)S(1)}, bf16[24,512]{1,0:T(8,128)(2,1)S(1)}, u32[]{:S(2)}, u32[]{:S(2)}) collective-permute-start(bf16[24,512]{1,0:T(8,128)(2,1)S(1)} %get-tuple-element.77), channel_id=1, source_target_pairs={{0,16},{1,24},{2,0},{3,8},{4,20},{5,28},{6,4},{7,12},{8,17},{9,25}... | collective-permute-start | bytes 73736 | tf_op jit(solution)/shard_map/ppermute | solution.py:465
  68.9 1.7 %collective-permute-start.21 = (bf16[24,512]{1,0:T(8,128)(2,1)S(1)}, bf16[24,512]{1,0:T(8,128)(2,1)S(1)}, u32[]{:S(2)}, u32[]{:S(2)}) collective-permute-start(bf16[24,512]{1,0:T(8,128)(2,1)S(1)} %get-tuple-element.76), channel_id=1, source_target_pairs={{0,20},{1,28},{2,4},{3,12},{4,16},{5,24},{6,0},{7,8},{8,21},{9,29}... | collective-permute-start | bytes 73736 | tf_op jit(solution)/shard_map/ppermute | solution.py:465
  71.4 2.2 %copy-done.1 = f32[8192,128]{1,0:T(8,128)S(1)} copy-done((f32[8192,128]{1,0:T(8,128)S(1)}, f32[8192,128]{1,0:T(8,128)}, u32[]{:S(2)}) %copy-start.1) | copy-done | bytes 4194328
  73.6 2.1 %flush.1 = f32[8192,128]{1,0:T(8,128)} custom-call(f32[8192,128]{1,0:T(8,128)S(1)} %copy-done.1), custom_call_target="tpu_custom_call" | custom-call | tf_op jit(solution)/shard_map/flush/pallas_call | solution.py:425
  (62 shorter events, 8.7 us)
Async XLA Ops:
  1.9 9.1 %collective-permute-start.1 = (bf16[24,4096]{1,0:T(8,128)(2,1)S(1)}, bf16[24,4096]{1,0:T(8,128)(2,1)S(1)}, u32[]{:S(2)}, u32[]{:S(2)}) collective-permute-start(bf16[24,4096]{1,0:T(8,128)(2,1)S(1)} %norm.1.refs_1_.refs_2_), channel_id=1, source_target_pairs={{16,0},{9,1},{18,2},{11,3},{20,4},{13,5},{22,6},{15,7},{24,8},{1,9... | collective-permute-start | bytes 589832 | tf_op jit(solution)/shard_map/ppermute | solution.py:248
  6.1 5.7 %collective-permute-start = (bf16[24,4096]{1,0:T(8,128)(2,1)S(1)}, bf16[24,4096]{1,0:T(8,128)(2,1)S(1)}, u32[]{:S(2)}, u32[]{:S(2)}) collective-permute-start(bf16[24,4096]{1,0:T(8,128)(2,1)S(1)} %norm.1.refs_1_.refs_2_), channel_id=1, source_target_pairs={{4,0},{5,1},{6,2},{7,3},{0,4},{1,5},{2,6},{3,7},{12,8},{13,9},{14,... | collective-permute-start | bytes 589832 | tf_op jit(solution)/shard_map/ppermute | solution.py:248
  7.6 1.6 %slice-start = ((bf16[4096,2,1,256]{3,1,2,0:T(2,128)(2,1)}), bf16[2048,2,1,256]{3,1,2,0:T(2,128)(2,1)S(1)}, s32[]{:S(2)}) async-start(bf16[4096,2,1,256]{3,1,2,0:T(2,128)(2,1)} %param.19), calls=%async_computation.1 | async-start | bytes 4194304 | tf_op jit(solution)/shard_map/slice | solution.py:258
  11.8 3.2 %slice-start.1 = ((bf16[4096,2,1,256]{3,1,2,0:T(2,128)(2,1)}), bf16[2048,2,1,256]{3,1,2,0:T(2,128)(2,1)S(1)}, s32[]{:S(2)}) async-start(bf16[4096,2,1,256]{3,1,2,0:T(2,128)(2,1)} %param.19), calls=%async_computation.2 | async-start | bytes 4194304 | tf_op jit(solution)/shard_map/slice | solution.py:262
  11.8 6.6 %collective-permute-start.3 = (bf16[24,4096]{1,0:T(8,128)(2,1)S(1)}, bf16[24,4096]{1,0:T(8,128)(2,1)S(1)}, u32[]{:S(2)}, u32[]{:S(2)}) collective-permute-start(bf16[24,4096]{1,0:T(8,128)(2,1)S(1)} %broadcast_select_fusion), channel_id=1, source_target_pairs={{8,0},{25,1},{10,2},{27,3},{12,4},{29,5},{14,6},{31,7},{0,8},{17,9... | collective-permute-start | bytes 589832 | tf_op jit(solution)/shard_map/ppermute | solution.py:248
  13.4 5.9 %collective-permute-start.2 = (bf16[24,4096]{1,0:T(8,128)(2,1)S(1)}, bf16[24,4096]{1,0:T(8,128)(2,1)S(1)}, u32[]{:S(2)}, u32[]{:S(2)}) collective-permute-start(bf16[24,4096]{1,0:T(8,128)(2,1)S(1)} %collective-permute-done.1.refs_4_), channel_id=1, source_target_pairs={{4,0},{5,1},{6,2},{7,3},{0,4},{1,5},{2,6},{3,7},{12,8},{13,9},{14,... | collective-permute-start | bytes 589832 | tf_op jit(solution)/shard_map/ppermute | solution.py:248
  14.9 6.5 %collective-permute-start.4 = (bf16[24,4096]{1,0:T(8,128)(2,1)S(1)}, bf16[24,4096]{1,0:T(8,128)(2,1)S(1)}, u32[]{:S(2)}, u32[]{:S(2)}) collective-permute-start(bf16[24,4096]{1,0:T(8,128)(2,1)S(1)} %collective-permute-done.1.refs_4_), channel_id=1, source_target_pairs={{0,1},{1,0},{2,3},{3,2},{4,5},{5,4},{6,7},{7,6},{8,9},{9,8},{10,11... | collective-permute-start | bytes 589832 | tf_op jit(solution)/shard_map/ppermute | solution.py:240
  19.3 2.1 %collective-permute-start.5 = (bf16[24,4096]{1,0:T(8,128)(2,1)S(1)}, bf16[24,4096]{1,0:T(8,128)(2,1)S(1)}, u32[]{:S(2)}, u32[]{:S(2)}) collective-permute-start(bf16[24,4096]{1,0:T(8,128)(2,1)S(1)} %collective-permute-done.2.refs_5_), channel_id=1, source_target_pairs={{0,1},{1,0},{2,3},{3,2},{4,5},{5,4},{6,7},{7,6},{8,9},{9,8},{10,11... | collective-permute-start | bytes 589832 | tf_op jit(solution)/shard_map/ppermute | solution.py:240
  19.3 2.1 %collective-permute-start.6 = (bf16[24,4096]{1,0:T(8,128)(2,1)S(1)}, bf16[24,4096]{1,0:T(8,128)(2,1)}, u32[]{:S(2)}, u32[]{:S(2)}) collective-permute-start(bf16[24,4096]{1,0:T(8,128)(2,1)S(1)} %collective-permute-done.3.refs_6_), channel_id=1, source_target_pairs={{0,1},{1,0},{2,3},{3,2},{4,5},{5,4},{6,7},{7,6},{8,9},{9,8},{10,11... | collective-permute-start | bytes 589832 | tf_op jit(solution)/shard_map/ppermute | solution.py:240
  21.5 8.2 %copy-start.4 = (s32[32]{0:T(128)S(1)}, s32[32]{0:T(128)}, u32[]{:S(2)}) copy-start(s32[32]{0:T(128)} %param.31) | copy-start | bytes 388
  21.5 9.7 %copy-start.2 = (s32[1,32]{1,0:T(1,128)S(1)}, s32[1,32]{1,0:T(1,128)}, u32[]{:S(2)}) copy-start(s32[1,32]{1,0:T(1,128)} %refs_6_.1) | copy-start | bytes 388
  24.1 13.0 %all-to-all-start = ((bf16[8,24,512]{2,1,0:T(8,128)(2,1)}), bf16[8,24,512]{2,1,0:T(8,128)(2,1)S(1)}, u32[]{:S(2)}, u32[]{:S(2)}) async-start(bf16[8,24,512]{2,1,0:T(8,128)(2,1)} %input.1.refs_5_), calls=%async_computation | async-start | bytes 393216 | tf_op jit(solution)/shard_map/all_to_all | solution.py:368
  37.6 4.7 %collective-permute-start.7 = (f32[32,288]{1,0:T(8,128)S(1)}, f32[32,288]{1,0:T(8,128)S(1)}, u32[]{:S(2)}, u32[]{:S(2)}) collective-permute-start(f32[32,288]{1,0:T(8,128)S(1)} %get-tuple-element.54.refs_5_.refs_0_), channel_id=1, source_target_pairs={{0,1},{1,0},{2,3},{3,2},{4,5},{5,4},{6,7},{7,6},{8,9},{9,8},{10,11... | collective-permute-start | bytes 110600 | tf_op jit(solution)/shard_map/ppermute | solution.py:240
  37.7 4.6 %collective-permute-start.8 = (f32[32,288]{1,0:T(8,128)S(1)}, f32[32,288]{1,0:T(8,128)S(1)}, u32[]{:S(2)}, u32[]{:S(2)}) collective-permute-start(f32[32,288]{1,0:T(8,128)S(1)} %get-tuple-element.54.refs_5_.refs_0_), channel_id=1, source_target_pairs={{0,2},{1,3},{2,0},{3,1},{4,6},{5,7},{6,4},{7,5},{8,10},{9,11},{10,... | collective-permute-start | bytes 110600 | tf_op jit(solution)/shard_map/ppermute | solution.py:240
  39.2 3.7 %collective-permute-start.9 = (f32[32,288]{1,0:T(8,128)S(1)}, f32[32,288]{1,0:T(8,128)S(1)}, u32[]{:S(2)}, u32[]{:S(2)}) collective-permute-start(f32[32,288]{1,0:T(8,128)S(1)} %get-tuple-element.54.refs_5_.refs_0_), channel_id=1, source_target_pairs={{0,3},{1,2},{2,1},{3,0},{4,7},{5,6},{6,5},{7,4},{8,11},{9,10},{10,... | collective-permute-start | bytes 110600 | tf_op jit(solution)/shard_map/ppermute | solution.py:240
  45.3 15.6 %copy-start = (f32[8192,128]{1,0:T(8,128)}, f32[8192,128]{1,0:T(8,128)S(1)}, u32[]{:S(2)}) copy-start(f32[8192,128]{1,0:T(8,128)S(1)} %get-tuple-element.70.source) | copy-start | bytes 12582916
  45.3 4.9 %collective-permute-start.10 = (bf16[24,2048]{1,0:T(8,128)(2,1)S(1)}, bf16[24,2048]{1,0:T(8,128)(2,1)S(1)}, u32[]{:S(2)}, u32[]{:S(2)}) collective-permute-start(bf16[24,2048]{1,0:T(8,128)(2,1)S(1)} %get-tuple-element.64.refs_2_), channel_id=1, source_target_pairs={{0,4},{4,0},{8,12},{12,8},{16,20},{20,16},{24,28},{28,24},{1,5},{5... | collective-permute-start | bytes 294920 | tf_op jit(solution)/shard_map/ppermute | solution.py:240
  46.3 7.4 %collective-permute-start.11 = (bf16[24,2048]{1,0:T(8,128)(2,1)S(1)}, bf16[24,2048]{1,0:T(8,128)(2,1)S(1)}, u32[]{:S(2)}, u32[]{:S(2)}) collective-permute-start(bf16[24,2048]{1,0:T(8,128)(2,1)S(1)} %get-tuple-element.64.refs_2_), channel_id=1, source_target_pairs={{0,16},{4,20},{8,24},{12,28},{16,0},{20,4},{24,8},{28,12},{1,17},{... | collective-permute-start | bytes 294920 | tf_op jit(solution)/shard_map/ppermute | solution.py:240
  46.4 9.8 %collective-permute-start.12 = (bf16[24,2048]{1,0:T(8,128)(2,1)S(1)}, bf16[24,2048]{1,0:T(8,128)(2,1)S(1)}, u32[]{:S(2)}, u32[]{:S(2)}) collective-permute-start(bf16[24,2048]{1,0:T(8,128)(2,1)S(1)} %get-tuple-element.64.refs_2_), channel_id=1, source_target_pairs={{0,8},{4,12},{8,0},{12,4},{16,24},{20,28},{24,16},{28,20},{1,9},{5... | collective-permute-start | bytes 294920 | tf_op jit(solution)/shard_map/ppermute | solution.py:240
  53.8 7.1 %collective-permute-start.14 = (bf16[24,2048]{1,0:T(8,128)(2,1)S(1)}, bf16[24,2048]{1,0:T(8,128)(2,1)S(1)}, u32[]{:S(2)}, u32[]{:S(2)}) collective-permute-start(bf16[24,2048]{1,0:T(8,128)(2,1)S(1)} %collective-permute-done.11), channel_id=1, source_target_pairs={{0,4},{4,0},{8,12},{12,8},{16,20},{20,16},{24,28},{28,24},{1,5},{5... | collective-permute-start | bytes 294920 | tf_op jit(solution)/shard_map/ppermute | solution.py:240
  54.7 6.7 %collective-permute-start.15 = (bf16[24,2048]{1,0:T(8,128)(2,1)S(1)}, bf16[24,2048]{1,0:T(8,128)(2,1)S(1)}, u32[]{:S(2)}, u32[]{:S(2)}) collective-permute-start(bf16[24,2048]{1,0:T(8,128)(2,1)S(1)} %collective-permute-done.11), channel_id=1, source_target_pairs={{0,8},{4,12},{8,0},{12,4},{16,24},{20,28},{24,16},{28,20},{1,9},{5... | collective-permute-start | bytes 294920 | tf_op jit(solution)/shard_map/ppermute | solution.py:240
  54.7 6.7 %collective-permute-start.16 = (bf16[24,2048]{1,0:T(8,128)(2,1)S(1)}, bf16[24,2048]{1,0:T(8,128)(2,1)S(1)}, u32[]{:S(2)}, u32[]{:S(2)}) collective-permute-start(bf16[24,2048]{1,0:T(8,128)(2,1)S(1)} %collective-permute-done.10), channel_id=1, source_target_pairs={{0,24},{4,28},{8,16},{12,20},{16,8},{20,12},{24,0},{28,4},{1,25},{... | collective-permute-start | bytes 294920 | tf_op jit(solution)/shard_map/ppermute | solution.py:240
  56.2 4.7 %collective-permute-start.13 = (bf16[24,2048]{1,0:T(8,128)(2,1)S(1)}, bf16[24,2048]{1,0:T(8,128)(2,1)S(1)}, u32[]{:S(2)}, u32[]{:S(2)}) collective-permute-start(bf16[24,2048]{1,0:T(8,128)(2,1)S(1)} %collective-permute-done.12), channel_id=1, source_target_pairs={{0,4},{4,0},{8,12},{12,8},{16,20},{20,16},{24,28},{28,24},{1,5},{5... | collective-permute-start | bytes 294920 | tf_op jit(solution)/shard_map/ppermute | solution.py:240
  60.9 3.3 %copy-start.3 = (bf16[32,3,2048]{2,0,1:T(8,128)(2,1)S(1)}, bf16[32,3,2048]{2,0,1:T(8,128)(2,1)}, u32[]{:S(2)}) copy-start(bf16[32,3,2048]{2,0,1:T(8,128)(2,1)} %param.29) | copy-start | bytes 1179652
  62.1 2.1 %collective-permute-start.17 = (bf16[48,512]{1,0:T(8,128)(2,1)S(1)}, bf16[48,512]{1,0:T(8,128)(2,1)S(1)}, u32[]{:S(2)}, u32[]{:S(2)}) collective-permute-start(bf16[48,512]{1,0:T(8,128)(2,1)S(1)} %get-tuple-element.71), channel_id=1, source_target_pairs={{0,1},{1,0},{2,3},{3,2},{4,5},{5,4},{6,7},{7,6},{8,9},{9,8},{10,11... | collective-permute-start | bytes 147464 | tf_op jit(solution)/shard_map/ppermute | solution.py:240
  62.2 4.3 %collective-permute-start.18 = (bf16[48,512]{1,0:T(8,128)(2,1)S(1)}, bf16[48,512]{1,0:T(8,128)(2,1)S(1)}, u32[]{:S(2)}, u32[]{:S(2)}) collective-permute-start(bf16[48,512]{1,0:T(8,128)(2,1)S(1)} %get-tuple-element.73), channel_id=1, source_target_pairs={{0,2},{1,3},{2,0},{3,1},{4,6},{5,7},{6,4},{7,5},{8,10},{9,11},{10,... | collective-permute-start | bytes 147464 | tf_op jit(solution)/shard_map/ppermute | solution.py:240
  63.2 3.9 %collective-permute-start.19 = (bf16[48,512]{1,0:T(8,128)(2,1)S(1)}, bf16[48,512]{1,0:T(8,128)(2,1)S(1)}, u32[]{:S(2)}, u32[]{:S(2)}) collective-permute-start(bf16[48,512]{1,0:T(8,128)(2,1)S(1)} %get-tuple-element.72), channel_id=1, source_target_pairs={{0,3},{1,2},{2,1},{3,0},{4,7},{5,6},{6,5},{7,4},{8,11},{9,10},{10,... | collective-permute-start | bytes 147464 | tf_op jit(solution)/shard_map/ppermute | solution.py:240
  67.2 8.5 %collective-permute-start.20 = (bf16[24,512]{1,0:T(8,128)(2,1)S(1)}, bf16[24,512]{1,0:T(8,128)(2,1)S(1)}, u32[]{:S(2)}, u32[]{:S(2)}) collective-permute-start(bf16[24,512]{1,0:T(8,128)(2,1)S(1)} %get-tuple-element.77), channel_id=1, source_target_pairs={{0,16},{1,24},{2,0},{3,8},{4,20},{5,28},{6,4},{7,12},{8,17},{9,25}... | collective-permute-start | bytes 73736 | tf_op jit(solution)/shard_map/ppermute | solution.py:465
  68.9 6.9 %collective-permute-start.21 = (bf16[24,512]{1,0:T(8,128)(2,1)S(1)}, bf16[24,512]{1,0:T(8,128)(2,1)S(1)}, u32[]{:S(2)}, u32[]{:S(2)}) collective-permute-start(bf16[24,512]{1,0:T(8,128)(2,1)S(1)} %get-tuple-element.76), channel_id=1, source_target_pairs={{0,20},{1,28},{2,4},{3,12},{4,16},{5,24},{6,0},{7,8},{8,21},{9,29}... | collective-permute-start | bytes 73736 | tf_op jit(solution)/shard_map/ppermute | solution.py:465
  71.4 2.2 %copy-start.1 = (f32[8192,128]{1,0:T(8,128)S(1)}, f32[8192,128]{1,0:T(8,128)}, u32[]{:S(2)}) copy-start(f32[8192,128]{1,0:T(8,128)} %copy-done) | copy-start | bytes 12582916

commit v2 on v1

--- a/solution.py
+++ b/solution.py
@@ -134,7 +134,7 @@
 
 
 def filter_kernel(spread, x_new, z_new, lengths, conv_state, conv_w, conv_b, w_dt_low, w_bc,
-                  packed, filtered, x_in, z_in):
+                  packed, sent, filtered, x_in, z_in):
     taps = conv_w.shape[0]
 
     def branch(ref, first):
@@ -161,6 +161,7 @@
     packed[:, rank:] = lax.dot_general(
         result, w_bc[...], (((1,), (1,)), ((), ())), preferred_element_type=F32
     )
+    sent[...] = packed[...].astype(BF16)
     z_in[...] = to_slots(branch(z_new, 1)).astype(BF16)
 
 
@@ -177,7 +178,7 @@
     active = live[...] > 0.5
     total = sums[0][...]
     for other in sums[1:]:
-        total = total + other[...]
+        total = total + other[...].astype(F32)
     rank = w_dt.shape[0]
     low = rms_rows(total[:, :rank], 1e-06).astype(BF16)
     b_in = rms_rows(total[:, rank : rank + count], 1e-06)
@@ -253,13 +254,13 @@
 
 def gather_shared(block, weights, fetch, t, n_dp, n_t):
     even = t % 2 == 0
-    deep = weights.shape[0] // 2
+    deep = weights.shape[0] * 7 // 16
     block, weights = lax.optimization_barrier((block, weights))
     upper = weights[:deep].reshape(deep, -1)
     side = swap_by_core(block, n_dp, n_t, (1, 1))
     far = swap_by_core(block, n_dp, n_t, (4, 2))
     far, upper, weights = lax.optimization_barrier((far, upper, weights))
-    lower = weights[deep:].reshape(deep, -1)
+    lower = weights[deep:].reshape(weights.shape[0] - deep, -1)
     far_side = swap_by_core(far, n_dp, n_t, (1, 1))
     last = swap_by_core(jnp.where(even, far, side), n_dp, n_t, (2, 6))
     upper, lower = lax.optimization_barrier((upper, lower))
@@ -272,8 +273,9 @@
 
 
 def gather_own(block, g, n_dp):
-    near, side = (swap_by(block, "dp", n_dp, m) for m in (2, 1))
     far = swap_by(block, "dp", n_dp, 4)
+    near = swap_by(block, "dp", n_dp, 2)
+    side = swap_by(block, "dp", n_dp, 1)
     side, far = lax.optimization_barrier((side, far))
     both = swap_by(far, "dp", n_dp, 2)
     near_side = swap_by(near, "dp", n_dp, 1)
@@ -370,8 +372,11 @@
         flat = slots * count * width // 128
         states = ssm_state.reshape(slots, count // 8, 8, width // 128, 128)
         states = jnp.transpose(states, (0, 1, 3, 2, 4)).reshape(flat, 128)
-        spread, pick, live, past_n, conv_w_n, conv_b_n, w_dt_low_n, w_bc_n = prefetch(
-            (past, conv_w, conv_b[None], w_dt_low, w_bc),
+        (
+            spread, pick, live, past_n, conv_w_n, conv_b_n, w_dt_low_n, w_bc_n, w_dt_n, bias_n,
+            a_log_n, skip_n,
+        ) = prefetch(
+            (past, conv_w, conv_b[None], w_dt_low, w_bc, w_dt, dt_bias[None], a_log, d_skip[None]),
             branches,
             near_out((slots, rows), BF16),
             near_out((rows, slots), BF16),
@@ -383,28 +388,27 @@
             owned = jnp.transpose(owned.reshape(n_dp, rows, 2, block), (2, 1, 0, 3))
             x_new, z_new = owned[0].reshape(rows, width), owned[1].reshape(rows, width)
         known = lengths[:, None]
-        packed, filtered, x_in, z_in = pl.pallas_call(
+        packed, sent, filtered, x_in, z_in = pl.pallas_call(
             filter_kernel,
             out_shape=(
                 near_out((slots, rank + 2 * count), F32),
+                near_out((slots, rank + 2 * count), BF16),
                 near_out((slots, width), BF16),
                 near_out((slots, width), BF16),
                 near_out((slots, width), BF16),
             ),
             in_specs=[VMEM] * 9,
-            out_specs=(VMEM,) * 4,
+            out_specs=(VMEM,) * 5,
             compiler_params=limit(8),
             name="filter",
         )(near(spread), near(x_new), near(z_new), near(known), near(past_n), near(conv_w_n),
           near(conv_b_n), near(w_dt_low_n), near(w_bc_n))
         if direct:
-            sums = [packed] + [swap_by(packed, "tensor", n_t, m) for m in range(1, n_t)]
+            sums = [packed] + [swap_by(sent, "tensor", n_t, m) for m in range(1, n_t)]
         else:
             sums = [lax.psum(packed, "tensor")]
-        w_dt_n, bias_n, a_log_n, skip_n, states_n = prefetch(
-            (w_dt, dt_bias[None], a_log, d_skip[None], states), packed
-        )
-        group, wide = 8, 2
+        (states_n,) = prefetch((states,), packed)
+        group, wide = 8, 4
         gated, states_next = pl.pallas_call(
             lambda *refs: state_kernel(*refs, parts=len(sums), group=group, wide=wide),
             out_shape=(near_out((rows, width), BF16), near_out((flat, 128), F32)),

time: 77.3 us -> 76.1 us (0.984)
  local copies, waits for them, and re-layouts: 9.33 us -> 7.49 us
  waiting for transfers between devices: 16.9 us -> 18.2 us
    ppermute x4, waiting for transfers between devices: 1.63 us -> 3.42 us  [swap_by_core(): return lax.ppermute(values, ('dp', 'tensor'), perm)]
    slice x2, local copies, waits for them, and re-layouts: 1.59 us -> 0.01 us  [gather_shared(): upper = weights[:deep].reshape(deep, -1)]
    pallas_call x1, Pallas kernels: 2.6 us -> 1.67 us  [body(): pl.pallas_call(lambda *refs: input_kernel(*refs, parts=n_dp), out_shape=o...]
  transfers between devices with their start and end apart: 23 -> 23, of which waited for: 10 -> 11; matrix products, arithmetic and copies ran while one was open for 8% -> 8% of each run, Pallas kernels for 15% -> 16%
where the time goes in v2:
time: 76.1 us; the launch traced here: 75.4 us
  starting transfers between devices  27.8 us (37%)
  Pallas kernels  18.5 us (24%)
  waiting for transfers between devices  18.2 us (24%)
  local copies, waits for them, and re-layouts  7.49 us (10%)
  between operations  1.69 us (2%)
  other arithmetic  1.02 us (1%)
    ppermute x16, waiting for transfers between devices, swap_by(): return lax.ppermute(values, axis, [(i, i ^ mask) for i in range(size)])  11.4 us
    ppermute x16, starting transfers between devices, swap_by(): return lax.ppermute(values, axis, [(i, i ^ mask) for i in range(size)])  10.9 us
    pallas_call x5, Pallas kernels, prefetch(): pl.pallas_call(lambda *refs: prefetch_kernel(*refs, parts=len(values)), o...  9.74 us
    ppermute x4, starting transfers between devices, swap_by_core(): return lax.ppermute(values, ('dp', 'tensor'), perm)  8.81 us
    unnamed x12, local copies, waits for them, and re-layouts  5.68 us
    all_to_all x1, starting transfers between devices, body(): lax.all_to_all(branches, 'dp', split_axis=0, concat_axis=0, tiled=True)  4.88 us
    all_to_all x1, waiting for transfers between devices, body(): lax.all_to_all(branches, 'dp', split_axis=0, concat_axis=0, tiled=True)  3.46 us
    ppermute x4, waiting for transfers between devices, swap_by_core(): return lax.ppermute(values, ('dp', 'tensor'), perm)  3.42 us
  transfers between devices with their start and end apart: 23, of which 11 were waited for; matrix products, arithmetic and copies ran while one was open for 8% of the time, Pallas kernels for 16%

profile of v2, /device:TPU:0, one launch (start us, length us, event | category | flops | bytes accessed | tf_op | source)
XLA Modules:
  0.0 75.4 jit_solution(12974102106189385157)
XLA Ops:
  0.6 1.4 %norm.1.refs_1_.refs_2_ = bf16[24,4096]{1,0:T(8,128)(2,1)S(1)} custom-call(s32[1,32]{1,0:T(1,128)} %refs_10_.1, bf16[32,4096]{1,0:T(8,128)(2,1)} %hidden_hbm.1, f32[1,4096]{1,0:T(1,128)} %bitcast.63), custom_call_target="tpu_custom_call" | custom-call | tf_op jit(solution)/shard_map/norm/pallas_call | solution.py:318
  2.1 4.1 %collective-permute-start.1 = (bf16[24,4096]{1,0:T(8,128)(2,1)S(1)}, bf16[24,4096]{1,0:T(8,128)(2,1)S(1)}, u32[]{:S(2)}, u32[]{:S(2)}) collective-permute-start(bf16[24,4096]{1,0:T(8,128)(2,1)S(1)} %norm.1.refs_1_.refs_2_), channel_id=1, source_target_pairs={{16,0},{9,1},{18,2},{11,3},{20,4},{13,5},{22,6},{15,7},{24,8},{1,9... | collective-permute-start | bytes 589832 | tf_op jit(solution)/shard_map/ppermute | solution.py:249
  6.2 1.5 %collective-permute-start = (bf16[24,4096]{1,0:T(8,128)(2,1)S(1)}, bf16[24,4096]{1,0:T(8,128)(2,1)S(1)}, u32[]{:S(2)}, u32[]{:S(2)}) collective-permute-start(bf16[24,4096]{1,0:T(8,128)(2,1)S(1)} %norm.1.refs_1_.refs_2_), channel_id=1, source_target_pairs={{4,0},{5,1},{6,2},{7,3},{0,4},{1,5},{2,6},{3,7},{12,8},{13,9},{14,... | collective-permute-start | bytes 589832 | tf_op jit(solution)/shard_map/ppermute | solution.py:249
  7.7 1.6 %copy.24 = bf16[224,8,2,256]{3,1,2,0:T(8,128)(2,1)} copy(bf16[224,8,2,256]{3,2,1,0:T(2,128)(2,1)S(1)} %bitcast.55) | data formatting | bytes 3670016
  9.4 1.3 %collective-permute-done.1.refs_4_ = bf16[24,4096]{1,0:T(8,128)(2,1)S(1)} collective-permute-done((bf16[24,4096]{1,0:T(8,128)(2,1)S(1)}, bf16[24,4096]{1,0:T(8,128)(2,1)S(1)}, u32[]{:S(2)}, u32[]{:S(2)}) %collective-permute-start.1) | collective-permute-done | bytes 196640 | tf_op jit(solution)/shard_map/ppermute | solution.py:249
  10.7 1.2 %collective-permute-done.refs_3_ = bf16[24,4096]{1,0:T(8,128)(2,1)S(1)} collective-permute-done((bf16[24,4096]{1,0:T(8,128)(2,1)S(1)}, bf16[24,4096]{1,0:T(8,128)(2,1)S(1)}, u32[]{:S(2)}, u32[]{:S(2)}) %collective-permute-start) | collective-permute-done | bytes 196640 | tf_op jit(solution)/shard_map/ppermute | solution.py:249
  11.9 1.6 %collective-permute-start.3 = (bf16[24,4096]{1,0:T(8,128)(2,1)S(1)}, bf16[24,4096]{1,0:T(8,128)(2,1)S(1)}, u32[]{:S(2)}, u32[]{:S(2)}) collective-permute-start(bf16[24,4096]{1,0:T(8,128)(2,1)S(1)} %broadcast_select_fusion), channel_id=1, source_target_pairs={{8,0},{25,1},{10,2},{27,3},{12,4},{29,5},{14,6},{31,7},{0,8},{17,9... | collective-permute-start | bytes 589832 | tf_op jit(solution)/shard_map/ppermute | solution.py:249
  13.6 1.5 %collective-permute-start.2 = (bf16[24,4096]{1,0:T(8,128)(2,1)S(1)}, bf16[24,4096]{1,0:T(8,128)(2,1)S(1)}, u32[]{:S(2)}, u32[]{:S(2)}) collective-permute-start(bf16[24,4096]{1,0:T(8,128)(2,1)S(1)} %collective-permute-done.1.refs_4_), channel_id=1, source_target_pairs={{4,0},{5,1},{6,2},{7,3},{0,4},{1,5},{2,6},{3,7},{12,8},{13,9},{14,... | collective-permute-start | bytes 589832 | tf_op jit(solution)/shard_map/ppermute | solution.py:249
  15.1 1.8 %copy.25 = bf16[288,8,2,256]{3,1,2,0:T(8,128)(2,1)} copy(bf16[288,8,2,256]{3,2,1,0:T(2,128)(2,1)S(1)} %bitcast.56) | data formatting | bytes 4718592
  16.9 1.6 %prefetch.5.refs_10_ = bf16[1792,512]{1,0:T(8,128)(2,1)S(1)} custom-call(bf16[1792,512]{1,0:T(8,128)(2,1)} %bitcast.57, bf16[24,4096]{1,0:T(8,128)(2,1)S(1)} %norm.1.refs_1_.refs_2_), custom_call_target="tpu_custom_call" | custom-call | tf_op jit(solution)/shard_map/prefetch/pallas_call | solution.py:334
  20.0 1.8 %prefetch.6.refs_11_ = bf16[2304,512]{1,0:T(8,128)(2,1)S(1)} custom-call(bf16[2304,512]{1,0:T(8,128)(2,1)} %bitcast.54, bf16[24,4096]{1,0:T(8,128)(2,1)S(1)} %norm.1.refs_1_.refs_2_), custom_call_target="tpu_custom_call" | custom-call | tf_op jit(solution)/shard_map/prefetch/pallas_call | solution.py:334
  21.9 1.7 %input.1.refs_9_ = bf16[8,24,512]{2,1,0:T(8,128)(2,1)} custom-call(s32[1]{0:T(128)} %bitcast.4.refs_0_, s32[1]{0:T(128)} %bitcast.5.refs_1_, bf16[24,4096]{1,0:T(8,128)(2,1)S(1)} %norm.1.refs_1_.refs_2_, bf16[24,4096]{1,0:T(8,128)(2,1)S(1)} %collective-permute-done.refs_3_, bf16[24,4096]{1,0:T(8,128)(2,1)S(1)} %collective-permute-done.1.refs_4_, ...), custom_call_target="tpu_custom_call" | custom-call | tf_op jit(solution)/shard_map/input/pallas_call | solution.py:355
  23.6 4.9 %all-to-all-start = ((bf16[8,24,512]{2,1,0:T(8,128)(2,1)}), bf16[8,24,512]{2,1,0:T(8,128)(2,1)S(1)}, u32[]{:S(2)}, u32[]{:S(2)}) async-start(bf16[8,24,512]{2,1,0:T(8,128)(2,1)} %input.1.refs_9_), calls=%async_computation | async-start | bytes 393216 | tf_op jit(solution)/shard_map/all_to_all | solution.py:370
  29.2 1.5 %constant_dynamic-slice_fusion.5.refs_1_ = bf16[32,1024]{1,0:T(8,128)(2,1)} fusion(bf16[32,4096]{1,0:T(8,128)(2,1)} %hidden_hbm.1, s32[]{:T(128)S(6)} %select_n.84), kind=kLoop, calls=%fused_computation.23 | loop fusion | bytes 131076 | tf_op jit(solution)/shard_map/dynamic_slice | solution.py:445
  30.7 2.4 %prefetch.7 = (bf16[32,24]{1,0:T(8,128)(2,1)S(1)}, bf16[24,32]{1,0:T(8,128)(2,1)S(1)}, f32[32,1]{1,0:T(8,128)S(1)}, bf16[3,32,2048]{2,1,0:T(8,128)(2,1)S(1)}, f3...) custom-call(bf16[3,32,2048]{2,1,0:T(8,128)(2,1)} %bitcast.61, ...), custom_call_target="tpu_custom_call" | custom-call | tf_op jit(solution)/shard_map/prefetch/pallas_call | solution.py:334
  33.1 3.5 %all-to-all-done.x_new.z_new = bf16[8,24,512]{2,1,0:T(8,128)(2,1)S(1)} async-done(((bf16[8,24,512]{2,1,0:T(8,128)(2,1)}), bf16[8,24,512]{2,1,0:T(8,128)(2,1)S(1)}, u32[]{:S(2)}, u32[]{:S(2)}) %all-to-all-start) | async-done | bytes 196640 | tf_op jit(solution)/shard_map/all_to_all | solution.py:370
  37.2 1.6 %collective-permute-start.8 = (bf16[32,288]{1,0:T(8,128)(2,1)S(1)}, bf16[32,288]{1,0:T(8,128)(2,1)S(1)}, u32[]{:S(2)}, u32[]{:S(2)}) collective-permute-start(bf16[32,288]{1,0:T(8,128)(2,1)S(1)} %get-tuple-element.55), channel_id=1, source_target_pairs={{0,2},{1,3},{2,0},{3,1},{4,6},{5,7},{6,4},{7,5},{8,10},{9,11},{10,... | collective-permute-start | bytes 55304 | tf_op jit(solution)/shard_map/ppermute | solution.py:241
  39.0 2.3 %prefetch.8.refs_13_ = f32[8192,128]{1,0:T(8,128)S(1)} custom-call(f32[8192,128]{1,0:T(8,128)} %bitcast.58, f32[32,288]{1,0:T(8,128)S(1)} %get-tuple-element.54.refs_1_.refs_0_), custom_call_target="tpu_custom_call" | custom-call | tf_op jit(solution)/shard_map/prefetch/pallas_call | solution.py:334
  42.0 2.3 %state.1 = (bf16[24,2048]{1,0:T(8,128)(2,1)S(1)}, f32[8192,128]{1,0:T(8,128)S(1)}) custom-call(f32[32,288]{1,0:T(8,128)S(1)} %get-tuple-element.54.refs_1_.refs_0_, bf16[32,288]{1,0:T(8,128)(2,1)S(1)} %collective-permute-done.7.refs_1_, bf16[32,288]{1,0:T(8,128)(2,1)S(1)} %collective-permute-done.8.refs_2_, ...), custom_call_target="tpu_custom_call" | custom-call | tf_op jit(solution)/shard_map/state/pallas_call | solution.py:412
  44.3 1.0 %collective-permute-start.10 = (bf16[24,2048]{1,0:T(8,128)(2,1)S(1)}, bf16[24,2048]{1,0:T(8,128)(2,1)S(1)}, u32[]{:S(2)}, u32[]{:S(2)}) collective-permute-start(bf16[24,2048]{1,0:T(8,128)(2,1)S(1)} %get-tuple-element.64.refs_2_), channel_id=1, source_target_pairs={{0,4},{4,0},{8,12},{12,8},{16,20},{20,16},{24,28},{28,24},{1,5},{5... | collective-permute-start | bytes 294920 | tf_op jit(solution)/shard_map/ppermute | solution.py:241
  45.3 2.0 %collective-permute-start.12 = (bf16[24,2048]{1,0:T(8,128)(2,1)S(1)}, bf16[24,2048]{1,0:T(8,128)(2,1)S(1)}, u32[]{:S(2)}, u32[]{:S(2)}) collective-permute-start(bf16[24,2048]{1,0:T(8,128)(2,1)S(1)} %get-tuple-element.64.refs_2_), channel_id=1, source_target_pairs={{0,8},{4,12},{8,0},{12,4},{16,24},{20,28},{24,16},{28,20},{1,9},{5... | collective-permute-start | bytes 294920 | tf_op jit(solution)/shard_map/ppermute | solution.py:241
  47.4 1.6 %prefetch.9 = (bf16[2048,512]{1,0:T(8,128)(2,1)S(1)}, bf16[32,1024]{1,0:T(8,128)(2,1)S(1)}) custom-call(bf16[2048,512]{1,0:T(8,128)(2,1)} %refs_0_.1, bf16[32,1024]{1,0:T(8,128)(2,1)} %constant_dynamic-slice_fusion.5.refs_1_, bf16[24,2048]{1,0:T(8,128)(2,1)S(1)} %get-tuple-element.64.refs_2_), custom_call_target="tpu_custom_call" | custom-call | tf_op jit(solution)/shard_map/prefetch/pallas_call | solution.py:334
  49.2 3.6 %collective-permute-done.11 = bf16[24,2048]{1,0:T(8,128)(2,1)S(1)} collective-permute-done((bf16[24,2048]{1,0:T(8,128)(2,1)S(1)}, bf16[24,2048]{1,0:T(8,128)(2,1)S(1)}, u32[]{:S(2)}, u32[]{:S(2)}) %collective-permute-start.11) | collective-permute-done | bytes 98336 | tf_op jit(solution)/shard_map/ppermute | solution.py:241
  53.6 1.4 %collective-permute-start.16 = (bf16[24,2048]{1,0:T(8,128)(2,1)S(1)}, bf16[24,2048]{1,0:T(8,128)(2,1)S(1)}, u32[]{:S(2)}, u32[]{:S(2)}) collective-permute-start(bf16[24,2048]{1,0:T(8,128)(2,1)S(1)} %collective-permute-done.10), channel_id=1, source_target_pairs={{0,24},{4,28},{8,16},{12,20},{16,8},{20,12},{24,0},{28,4},{1,25},{... | collective-permute-start | bytes 294920 | tf_op jit(solution)/shard_map/ppermute | solution.py:241
  55.1 1.2 %collective-permute-start.13 = (bf16[24,2048]{1,0:T(8,128)(2,1)S(1)}, bf16[24,2048]{1,0:T(8,128)(2,1)S(1)}, u32[]{:S(2)}, u32[]{:S(2)}) collective-permute-start(bf16[24,2048]{1,0:T(8,128)(2,1)S(1)} %collective-permute-done.12), channel_id=1, source_target_pairs={{0,4},{4,0},{8,12},{12,8},{16,20},{20,16},{24,28},{28,24},{1,5},{5... | collective-permute-start | bytes 294920 | tf_op jit(solution)/shard_map/ppermute | solution.py:241
  56.3 3.5 %collective-permute-done.13 = bf16[24,2048]{1,0:T(8,128)(2,1)S(1)} collective-permute-done((bf16[24,2048]{1,0:T(8,128)(2,1)S(1)}, bf16[24,2048]{1,0:T(8,128)(2,1)S(1)}, u32[]{:S(2)}, u32[]{:S(2)}) %collective-permute-start.13) | collective-permute-done | bytes 98336 | tf_op jit(solution)/shard_map/ppermute | solution.py:241
  61.1 1.0 %collective-permute-start.18 = (bf16[48,512]{1,0:T(8,128)(2,1)S(1)}, bf16[48,512]{1,0:T(8,128)(2,1)S(1)}, u32[]{:S(2)}, u32[]{:S(2)}) collective-permute-start(bf16[48,512]{1,0:T(8,128)(2,1)S(1)} %get-tuple-element.73), channel_id=1, source_target_pairs={{0,2},{1,3},{2,0},{3,1},{4,6},{5,7},{6,4},{7,5},{8,10},{9,11},{10,... | collective-permute-start | bytes 147464 | tf_op jit(solution)/shard_map/ppermute | solution.py:241
  63.1 2.3 %collective-permute-done.18 = bf16[48,512]{1,0:T(8,128)(2,1)S(1)} collective-permute-done((bf16[48,512]{1,0:T(8,128)(2,1)S(1)}, bf16[48,512]{1,0:T(8,128)(2,1)S(1)}, u32[]{:S(2)}, u32[]{:S(2)}) %collective-permute-start.18) | collective-permute-done | bytes 49184 | tf_op jit(solution)/shard_map/ppermute | solution.py:241
  66.2 1.6 %collective-permute-start.20 = (bf16[24,512]{1,0:T(8,128)(2,1)S(1)}, bf16[24,512]{1,0:T(8,128)(2,1)S(1)}, u32[]{:S(2)}, u32[]{:S(2)}) collective-permute-start(bf16[24,512]{1,0:T(8,128)(2,1)S(1)} %get-tuple-element.77), channel_id=1, source_target_pairs={{0,16},{1,24},{2,0},{3,8},{4,20},{5,28},{6,4},{7,12},{8,17},{9,25}... | collective-permute-start | bytes 73736 | tf_op jit(solution)/shard_map/ppermute | solution.py:469
  67.8 1.6 %collective-permute-start.21 = (bf16[24,512]{1,0:T(8,128)(2,1)S(1)}, bf16[24,512]{1,0:T(8,128)(2,1)S(1)}, u32[]{:S(2)}, u32[]{:S(2)}) collective-permute-start(bf16[24,512]{1,0:T(8,128)(2,1)S(1)} %get-tuple-element.76), channel_id=1, source_target_pairs={{0,20},{1,28},{2,4},{3,12},{4,16},{5,24},{6,0},{7,8},{8,21},{9,29}... | collective-permute-start | bytes 73736 | tf_op jit(solution)/shard_map/ppermute | solution.py:469
  70.2 2.2 %copy-done.1 = f32[8192,128]{1,0:T(8,128)S(1)} copy-done((f32[8192,128]{1,0:T(8,128)S(1)}, f32[8192,128]{1,0:T(8,128)}, u32[]{:S(2)}) %copy-start.1) | copy-done | bytes 4194328
  72.4 2.1 %flush.1 = f32[8192,128]{1,0:T(8,128)} custom-call(f32[8192,128]{1,0:T(8,128)S(1)} %copy-done.1), custom_call_target="tpu_custom_call" | custom-call | tf_op jit(solution)/shard_map/flush/pallas_call | solution.py:429
  (62 shorter events, 8.9 us)
Async XLA Ops:
  0.6 7.1 %slice-start = ((bf16[4096,2,1,256]{3,1,2,0:T(2,128)(2,1)}), bf16[1792,2,1,256]{3,1,2,0:T(2,128)(2,1)S(1)}, s32[]{:S(2)}) async-start(bf16[4096,2,1,256]{3,1,2,0:T(2,128)(2,1)} %param.19), calls=%async_computation.1 | async-start | bytes 3670016 | tf_op jit(solution)/shard_map/slice | solution.py:259
  2.1 8.6 %collective-permute-start.1 = (bf16[24,4096]{1,0:T(8,128)(2,1)S(1)}, bf16[24,4096]{1,0:T(8,128)(2,1)S(1)}, u32[]{:S(2)}, u32[]{:S(2)}) collective-permute-start(bf16[24,4096]{1,0:T(8,128)(2,1)S(1)} %norm.1.refs_1_.refs_2_), channel_id=1, source_target_pairs={{16,0},{9,1},{18,2},{11,3},{20,4},{13,5},{22,6},{15,7},{24,8},{1,9... | collective-permute-start | bytes 589832 | tf_op jit(solution)/shard_map/ppermute | solution.py:249
  6.2 5.7 %collective-permute-start = (bf16[24,4096]{1,0:T(8,128)(2,1)S(1)}, bf16[24,4096]{1,0:T(8,128)(2,1)S(1)}, u32[]{:S(2)}, u32[]{:S(2)}) collective-permute-start(bf16[24,4096]{1,0:T(8,128)(2,1)S(1)} %norm.1.refs_1_.refs_2_), channel_id=1, source_target_pairs={{4,0},{5,1},{6,2},{7,3},{0,4},{1,5},{2,6},{3,7},{12,8},{13,9},{14,... | collective-permute-start | bytes 589832 | tf_op jit(solution)/shard_map/ppermute | solution.py:249
  11.9 3.2 %slice-start.1 = ((bf16[4096,2,1,256]{3,1,2,0:T(2,128)(2,1)}), bf16[2304,2,1,256]{3,1,2,0:T(2,128)(2,1)S(1)}, s32[]{:S(2)}) async-start(bf16[4096,2,1,256]{3,1,2,0:T(2,128)(2,1)} %param.19), calls=%async_computation.2 | async-start | bytes 4718592 | tf_op jit(solution)/shard_map/slice | solution.py:263
  11.9 6.6 %collective-permute-start.3 = (bf16[24,4096]{1,0:T(8,128)(2,1)S(1)}, bf16[24,4096]{1,0:T(8,128)(2,1)S(1)}, u32[]{:S(2)}, u32[]{:S(2)}) collective-permute-start(bf16[24,4096]{1,0:T(8,128)(2,1)S(1)} %broadcast_select_fusion), channel_id=1, source_target_pairs={{8,0},{25,1},{10,2},{27,3},{12,4},{29,5},{14,6},{31,7},{0,8},{17,9... | collective-permute-start | bytes 589832 | tf_op jit(solution)/shard_map/ppermute | solution.py:249
  13.6 5.9 %collective-permute-start.2 = (bf16[24,4096]{1,0:T(8,128)(2,1)S(1)}, bf16[24,4096]{1,0:T(8,128)(2,1)S(1)}, u32[]{:S(2)}, u32[]{:S(2)}) collective-permute-start(bf16[24,4096]{1,0:T(8,128)(2,1)S(1)} %collective-permute-done.1.refs_4_), channel_id=1, source_target_pairs={{4,0},{5,1},{6,2},{7,3},{0,4},{1,5},{2,6},{3,7},{12,8},{13,9},{14,... | collective-permute-start | bytes 589832 | tf_op jit(solution)/shard_map/ppermute | solution.py:249
  15.1 6.7 %collective-permute-start.4 = (bf16[24,4096]{1,0:T(8,128)(2,1)S(1)}, bf16[24,4096]{1,0:T(8,128)(2,1)S(1)}, u32[]{:S(2)}, u32[]{:S(2)}) collective-permute-start(bf16[24,4096]{1,0:T(8,128)(2,1)S(1)} %collective-permute-done.1.refs_4_), channel_id=1, source_target_pairs={{0,1},{1,0},{2,3},{3,2},{4,5},{5,4},{6,7},{7,6},{8,9},{9,8},{10,11... | collective-permute-start | bytes 589832 | tf_op jit(solution)/shard_map/ppermute | solution.py:241
  19.5 2.4 %collective-permute-start.5 = (bf16[24,4096]{1,0:T(8,128)(2,1)S(1)}, bf16[24,4096]{1,0:T(8,128)(2,1)S(1)}, u32[]{:S(2)}, u32[]{:S(2)}) collective-permute-start(bf16[24,4096]{1,0:T(8,128)(2,1)S(1)} %collective-permute-done.2.refs_5_), channel_id=1, source_target_pairs={{0,1},{1,0},{2,3},{3,2},{4,5},{5,4},{6,7},{7,6},{8,9},{9,8},{10,11... | collective-permute-start | bytes 589832 | tf_op jit(solution)/shard_map/ppermute | solution.py:241
  19.5 2.4 %collective-permute-start.6 = (bf16[24,4096]{1,0:T(8,128)(2,1)S(1)}, bf16[24,4096]{1,0:T(8,128)(2,1)S(1)}, u32[]{:S(2)}, u32[]{:S(2)}) collective-permute-start(bf16[24,4096]{1,0:T(8,128)(2,1)S(1)} %collective-permute-done.3.refs_6_), channel_id=1, source_target_pairs={{0,1},{1,0},{2,3},{3,2},{4,5},{5,4},{6,7},{7,6},{8,9},{9,8},{10,11... | collective-permute-start | bytes 589832 | tf_op jit(solution)/shard_map/ppermute | solution.py:241
  21.9 7.2 %copy-start.4 = (s32[32]{0:T(128)S(1)}, s32[32]{0:T(128)}, u32[]{:S(2)}) copy-start(s32[32]{0:T(128)} %param.31) | copy-start | bytes 388
  21.9 8.8 %copy-start.2 = (s32[1,32]{1,0:T(1,128)S(1)}, s32[1,32]{1,0:T(1,128)}, u32[]{:S(2)}) copy-start(s32[1,32]{1,0:T(1,128)} %refs_10_.1) | copy-start | bytes 388
  23.6 13.0 %all-to-all-start = ((bf16[8,24,512]{2,1,0:T(8,128)(2,1)}), bf16[8,24,512]{2,1,0:T(8,128)(2,1)S(1)}, u32[]{:S(2)}, u32[]{:S(2)}) async-start(bf16[8,24,512]{2,1,0:T(8,128)(2,1)} %input.1.refs_9_), calls=%async_computation | async-start | bytes 393216 | tf_op jit(solution)/shard_map/all_to_all | solution.py:370
  37.1 4.2 %collective-permute-start.7 = (bf16[32,288]{1,0:T(8,128)(2,1)S(1)}, bf16[32,288]{1,0:T(8,128)(2,1)S(1)}, u32[]{:S(2)}, u32[]{:S(2)}) collective-permute-start(bf16[32,288]{1,0:T(8,128)(2,1)S(1)} %get-tuple-element.55), channel_id=1, source_target_pairs={{0,1},{1,0},{2,3},{3,2},{4,5},{5,4},{6,7},{7,6},{8,9},{9,8},{10,11... | collective-permute-start | bytes 55304 | tf_op jit(solution)/shard_map/ppermute | solution.py:241
  37.2 4.1 %collective-permute-start.8 = (bf16[32,288]{1,0:T(8,128)(2,1)S(1)}, bf16[32,288]{1,0:T(8,128)(2,1)S(1)}, u32[]{:S(2)}, u32[]{:S(2)}) collective-permute-start(bf16[32,288]{1,0:T(8,128)(2,1)S(1)} %get-tuple-element.55), channel_id=1, source_target_pairs={{0,2},{1,3},{2,0},{3,1},{4,6},{5,7},{6,4},{7,5},{8,10},{9,11},{10,... | collective-permute-start | bytes 55304 | tf_op jit(solution)/shard_map/ppermute | solution.py:241
  38.7 3.3 %collective-permute-start.9 = (bf16[32,288]{1,0:T(8,128)(2,1)S(1)}, bf16[32,288]{1,0:T(8,128)(2,1)S(1)}, u32[]{:S(2)}, u32[]{:S(2)}) collective-permute-start(bf16[32,288]{1,0:T(8,128)(2,1)S(1)} %get-tuple-element.55), channel_id=1, source_target_pairs={{0,3},{1,2},{2,1},{3,0},{4,7},{5,6},{6,5},{7,4},{8,11},{9,10},{10,... | collective-permute-start | bytes 55304 | tf_op jit(solution)/shard_map/ppermute | solution.py:241
  44.2 16.8 %copy-start = (f32[8192,128]{1,0:T(8,128)}, f32[8192,128]{1,0:T(8,128)S(1)}, u32[]{:S(2)}) copy-start(f32[8192,128]{1,0:T(8,128)S(1)} %get-tuple-element.70.source) | copy-start | bytes 12582916
  44.3 4.9 %collective-permute-start.10 = (bf16[24,2048]{1,0:T(8,128)(2,1)S(1)}, bf16[24,2048]{1,0:T(8,128)(2,1)S(1)}, u32[]{:S(2)}, u32[]{:S(2)}) collective-permute-start(bf16[24,2048]{1,0:T(8,128)(2,1)S(1)} %get-tuple-element.64.refs_2_), channel_id=1, source_target_pairs={{0,4},{4,0},{8,12},{12,8},{16,20},{20,16},{24,28},{28,24},{1,5},{5... | collective-permute-start | bytes 294920 | tf_op jit(solution)/shard_map/ppermute | solution.py:241
  45.3 7.4 %collective-permute-start.11 = (bf16[24,2048]{1,0:T(8,128)(2,1)S(1)}, bf16[24,2048]{1,0:T(8,128)(2,1)S(1)}, u32[]{:S(2)}, u32[]{:S(2)}) collective-permute-start(bf16[24,2048]{1,0:T(8,128)(2,1)S(1)} %get-tuple-element.64.refs_2_), channel_id=1, source_target_pairs={{0,16},{4,20},{8,24},{12,28},{16,0},{20,4},{24,8},{28,12},{1,17},{... | collective-permute-start | bytes 294920 | tf_op jit(solution)/shard_map/ppermute | solution.py:241
  45.3 9.8 %collective-permute-start.12 = (bf16[24,2048]{1,0:T(8,128)(2,1)S(1)}, bf16[24,2048]{1,0:T(8,128)(2,1)S(1)}, u32[]{:S(2)}, u32[]{:S(2)}) collective-permute-start(bf16[24,2048]{1,0:T(8,128)(2,1)S(1)} %get-tuple-element.64.refs_2_), channel_id=1, source_target_pairs={{0,8},{4,12},{8,0},{12,4},{16,24},{20,28},{24,16},{28,20},{1,9},{5... | collective-permute-start | bytes 294920 | tf_op jit(solution)/shard_map/ppermute | solution.py:241
  49.0 14.1 %copy-start.3 = (bf16[32,3,2048]{2,0,1:T(8,128)(2,1)S(1)}, bf16[32,3,2048]{2,0,1:T(8,128)(2,1)}, u32[]{:S(2)}) copy-start(bf16[32,3,2048]{2,0,1:T(8,128)(2,1)} %param.29) | copy-start | bytes 1179652
  52.7 7.1 %collective-permute-start.14 = (bf16[24,2048]{1,0:T(8,128)(2,1)S(1)}, bf16[24,2048]{1,0:T(8,128)(2,1)S(1)}, u32[]{:S(2)}, u32[]{:S(2)}) collective-permute-start(bf16[24,2048]{1,0:T(8,128)(2,1)S(1)} %collective-permute-done.11), channel_id=1, source_target_pairs={{0,4},{4,0},{8,12},{12,8},{16,20},{20,16},{24,28},{28,24},{1,5},{5... | collective-permute-start | bytes 294920 | tf_op jit(solution)/shard_map/ppermute | solution.py:241
  53.6 6.7 %collective-permute-start.15 = (bf16[24,2048]{1,0:T(8,128)(2,1)S(1)}, bf16[24,2048]{1,0:T(8,128)(2,1)S(1)}, u32[]{:S(2)}, u32[]{:S(2)}) collective-permute-start(bf16[24,2048]{1,0:T(8,128)(2,1)S(1)} %collective-permute-done.11), channel_id=1, source_target_pairs={{0,8},{4,12},{8,0},{12,4},{16,24},{20,28},{24,16},{28,20},{1,9},{5... | collective-permute-start | bytes 294920 | tf_op jit(solution)/shard_map/ppermute | solution.py:241
  53.6 6.7 %collective-permute-start.16 = (bf16[24,2048]{1,0:T(8,128)(2,1)S(1)}, bf16[24,2048]{1,0:T(8,128)(2,1)S(1)}, u32[]{:S(2)}, u32[]{:S(2)}) collective-permute-start(bf16[24,2048]{1,0:T(8,128)(2,1)S(1)} %collective-permute-done.10), channel_id=1, source_target_pairs={{0,24},{4,28},{8,16},{12,20},{16,8},{20,12},{24,0},{28,4},{1,25},{... | collective-permute-start | bytes 294920 | tf_op jit(solution)/shard_map/ppermute | solution.py:241
  55.1 4.7 %collective-permute-start.13 = (bf16[24,2048]{1,0:T(8,128)(2,1)S(1)}, bf16[24,2048]{1,0:T(8,128)(2,1)S(1)}, u32[]{:S(2)}, u32[]{:S(2)}) collective-permute-start(bf16[24,2048]{1,0:T(8,128)(2,1)S(1)} %collective-permute-done.12), channel_id=1, source_target_pairs={{0,4},{4,0},{8,12},{12,8},{16,20},{20,16},{24,28},{28,24},{1,5},{5... | collective-permute-start | bytes 294920 | tf_op jit(solution)/shard_map/ppermute | solution.py:241
  61.0 2.1 %collective-permute-start.17 = (bf16[48,512]{1,0:T(8,128)(2,1)S(1)}, bf16[48,512]{1,0:T(8,128)(2,1)S(1)}, u32[]{:S(2)}, u32[]{:S(2)}) collective-permute-start(bf16[48,512]{1,0:T(8,128)(2,1)S(1)} %get-tuple-element.71), channel_id=1, source_target_pairs={{0,1},{1,0},{2,3},{3,2},{4,5},{5,4},{6,7},{7,6},{8,9},{9,8},{10,11... | collective-permute-start | bytes 147464 | tf_op jit(solution)/shard_map/ppermute | solution.py:241
  61.1 4.3 %collective-permute-start.18 = (bf16[48,512]{1,0:T(8,128)(2,1)S(1)}, bf16[48,512]{1,0:T(8,128)(2,1)S(1)}, u32[]{:S(2)}, u32[]{:S(2)}) collective-permute-start(bf16[48,512]{1,0:T(8,128)(2,1)S(1)} %get-tuple-element.73), channel_id=1, source_target_pairs={{0,2},{1,3},{2,0},{3,1},{4,6},{5,7},{6,4},{7,5},{8,10},{9,11},{10,... | collective-permute-start | bytes 147464 | tf_op jit(solution)/shard_map/ppermute | solution.py:241
  62.1 4.0 %collective-permute-start.19 = (bf16[48,512]{1,0:T(8,128)(2,1)S(1)}, bf16[48,512]{1,0:T(8,128)(2,1)S(1)}, u32[]{:S(2)}, u32[]{:S(2)}) collective-permute-start(bf16[48,512]{1,0:T(8,128)(2,1)S(1)} %get-tuple-element.72), channel_id=1, source_target_pairs={{0,3},{1,2},{2,1},{3,0},{4,7},{5,6},{6,5},{7,4},{8,11},{9,10},{10,... | collective-permute-start | bytes 147464 | tf_op jit(solution)/shard_map/ppermute | solution.py:241
  66.2 8.4 %collective-permute-start.20 = (bf16[24,512]{1,0:T(8,128)(2,1)S(1)}, bf16[24,512]{1,0:T(8,128)(2,1)S(1)}, u32[]{:S(2)}, u32[]{:S(2)}) collective-permute-start(bf16[24,512]{1,0:T(8,128)(2,1)S(1)} %get-tuple-element.77), channel_id=1, source_target_pairs={{0,16},{1,24},{2,0},{3,8},{4,20},{5,28},{6,4},{7,12},{8,17},{9,25}... | collective-permute-start | bytes 73736 | tf_op jit(solution)/shard_map/ppermute | solution.py:469
  67.8 6.8 %collective-permute-start.21 = (bf16[24,512]{1,0:T(8,128)(2,1)S(1)}, bf16[24,512]{1,0:T(8,128)(2,1)S(1)}, u32[]{:S(2)}, u32[]{:S(2)}) collective-permute-start(bf16[24,512]{1,0:T(8,128)(2,1)S(1)} %get-tuple-element.76), channel_id=1, source_target_pairs={{0,20},{1,28},{2,4},{3,12},{4,16},{5,24},{6,0},{7,8},{8,21},{9,29}... | collective-permute-start | bytes 73736 | tf_op jit(solution)/shard_map/ppermute | solution.py:469
  70.2 2.2 %copy-start.1 = (f32[8192,128]{1,0:T(8,128)S(1)}, f32[8192,128]{1,0:T(8,128)}, u32[]{:S(2)}) copy-start(f32[8192,128]{1,0:T(8,128)} %copy-done) | copy-start | bytes 12582916
